TPU v7x, 256 devices: a whole 4x4x8 slice. The times are simulated.
256 devices in a mesh: space: 8 (over z_hi, y), inner: 32 (over z_lo, x, core).
Axes of the slice: x: 4, y: 4, z: 8 (z_hi: 2, z_lo: 4; z = z_hi * 4 + z_lo), core: 2. Of those that a mesh axis runs over, the one named last changes fastest.
Arguments:
- hamiltonian: bfloat16 [512, 5, 128, 128], P(('space', 'inner')), as said below
- pattern: int32 [512, 5], P(('space', 'inner')), may hold values from 0 to 1, as said below
- ortho: bfloat16 [512, 2, 128, 128], P(('space', 'inner')), may hold values from -0.25 to 0.25
- lists: int32 [512, 6], P(('space', 'inner')), may hold values from -1 to 511, as said below
Outputs:
- density: float32 [512, 13, 128, 128], P(('space', 'inner'))
Inputs may be any that keep to these rules, and one draw needn't show every extreme that they name: Symmetric block band: hamiltonian[j, r] is the transpose of hamiltonian[j + r - 2, 4 - r]; blocks that point outside the matrix are zero. symmetric: pattern[j, r] equals pattern[j + r - 2, 4 - r]; the middle entry is 1; entries that point outside the matrix are 0. lists[j, 0] = j; the next entries are distinct block columns within 5 of j other than j, followed only by -1; each row has 3 to 6 entries that are not -1, and some row has 6.
All inputs are finite; a program needn't handle non-finite values.
Results may differ from a plain program's by a relative error of at most 0.0055.
Values may be sent and summed in bfloat16 or wider, within the bound.
No kernel may reach another device: no remote copies, remote signals or barrier semaphores. Data moves between devices by JAX's collectives and lax.ppermute only.
A program may use at most 64 MiB of HBM per device.

v0:
```python
import jax
import jax.numpy as jnp
import numpy as np
from jax import lax
from jax.sharding import PartitionSpec as P

RO = 3
Q = 5
STEPS = 3


chem_level = 0.25


def shifted_2(value, axis, by):
    length = lax.axis_size(axis)
    pairs = [(i, i + by) for i in range(length) if 0 <= i + by < length]
    return lax.ppermute(value, axis, pairs)


def orth_columns(ham_ext, ortho_ext, ham_off, ortho_off, count, first_row):
    column_range = np.arange(count)
    previous = ham_ext[ham_off + column_range - 1]
    current = ham_ext[ham_off + column_range]
    upper = ortho_ext[ortho_off + column_range, 0]
    diagonal = ortho_ext[ortho_off + column_range, 1]
    row_index = ortho_off + column_range[:, None] + np.arange(first_row - RO, RO + 1)[None, :]
    z_rows = ortho_ext[row_index]
    left_padded = jnp.pad(previous, ((0, 0), (1, 2), (0, 0), (0, 0)))[:, first_row:]
    right_padded = jnp.pad(current, ((0, 0), (2, 1), (0, 0), (0, 0)))[:, first_row:]
    product = jnp.einsum("cgab,cbd->cgad", left_padded, upper, preferred_element_type=jnp.float32)
    product = product + jnp.einsum(
        "cgab,cbd->cgad", right_padded, diagonal, preferred_element_type=jnp.float32
    )
    product = product.astype(jnp.bfloat16)
    result = jnp.einsum(
        "cqba,cqbd->cqad", z_rows[:, :, 0], product[:, :-1], preferred_element_type=jnp.float32
    )
    result = result + jnp.einsum(
        "cqba,cqbd->cqad", z_rows[:, :, 1], product[:, 1:], preferred_element_type=jnp.float32
    )
    return result.astype(jnp.bfloat16)


def mat_product(left, right):
    return jnp.dot(left, right, preferred_element_type=jnp.float32)


def solve_column(orth_ext, base, slots, column):
    positions = jnp.clip(slots - base, 0, orth_ext.shape[0] - 1).astype(jnp.int32)
    gathered = orth_ext[positions]
    first_row = 2 * RO + 1 - gathered.shape[1]
    live = slots >= 0
    both_live = live[:, None, None] & live[None, :, None]
    offsets_grid = slots[:, None] - slots[None, :] + RO
    band_rows = jnp.arange(first_row, 2 * RO + 1, dtype=jnp.int32)[None, None, :]
    lower_sel = (
        (offsets_grid[:, :, None] == band_rows) & (offsets_grid >= RO)[:, :, None] & both_live
    )
    upper_sel = (
        ((2 * RO - offsets_grid)[:, :, None] == band_rows)
        & (offsets_grid < RO)[:, :, None]
        & both_live
    )
    sub_block = jnp.einsum(
        "str,trab->satb",
        lower_sel.astype(jnp.bfloat16),
        gathered,
        preferred_element_type=jnp.float32,
    )
    sub_block = sub_block + jnp.einsum(
        "str,srba->satb",
        upper_sel.astype(jnp.bfloat16),
        gathered,
        preferred_element_type=jnp.float32,
    )
    slot_count = gathered.shape[0]
    block_size = gathered.shape[-1]
    order_n = slot_count * block_size
    sub_block = sub_block.reshape(order_n, order_n)
    diag_values = jnp.repeat(live.astype(jnp.float32), block_size)
    shifted = chem_level * jnp.diag(diag_values) - sub_block
    squares = jnp.sum(shifted * shifted)
    live_rows = jnp.sum(live.astype(jnp.float32)) * block_size
    scale = 2.0 * jnp.sqrt(squares / live_rows + 1e-06)
    iterate = (shifted / scale).astype(jnp.bfloat16)
    identity = jnp.eye(order_n, dtype=jnp.float32)
    for step_index in range(STEPS - 1):
        square = mat_product(iterate, iterate)
        factor = (1.5 * identity - 0.5 * square).astype(jnp.bfloat16)
        iterate = mat_product(iterate, factor).astype(jnp.bfloat16)
    columns = iterate[:, :block_size]
    unit = identity[:, :block_size]
    square_col = mat_product(iterate, columns)
    factor_col = (1.5 * unit - 0.5 * square_col).astype(jnp.bfloat16)
    result = mat_product(iterate, factor_col)
    pcol = (0.5 * (unit + result)).reshape(slot_count, block_size, block_size)
    placing = (
        ((slots - column + Q)[:, None] == jnp.arange(2 * Q + 1, dtype=jnp.int32)[None, :])
        & live[:, None]
    ).astype(jnp.float32)
    return jnp.einsum("sr,sab->rab", placing, pcol, precision=lax.Precision.HIGHEST)


def back_transform(porth, porth_next, ortho_ext, ortho_off, count):
    column_range = np.arange(count)
    diag_own = ortho_ext[ortho_off + column_range, 1].astype(jnp.float32)
    upper_next = ortho_ext[ortho_off + column_range + 1, 0].astype(jnp.float32)
    low_band = jnp.pad(porth, ((0, 0), (0, 1), (0, 0), (0, 0)))
    high_band = jnp.pad(porth_next, ((0, 0), (1, 0), (0, 0), (0, 0)))
    right_part = jnp.einsum("crab,cdb->crad", low_band, diag_own, precision=lax.Precision.HIGHEST)
    right_part = right_part + jnp.einsum(
        "crab,cdb->crad", high_band, upper_next, precision=lax.Precision.HIGHEST
    )
    row_index = ortho_off + column_range[:, None] + np.arange(-Q - 1, Q + 2)[None, :]
    diag_rows = ortho_ext[row_index, 1].astype(jnp.float32)
    upper_rows = ortho_ext[row_index + 1, 0].astype(jnp.float32)
    lower_y = jnp.pad(right_part, ((0, 0), (1, 0), (0, 0), (0, 0)))
    upper_y = jnp.pad(right_part, ((0, 0), (0, 1), (0, 0), (0, 0)))
    result = jnp.einsum("cpab,cpbd->cpad", diag_rows, lower_y, precision=lax.Precision.HIGHEST)
    return result + jnp.einsum(
        "cpab,cpbd->cpad", upper_rows, upper_y, precision=lax.Precision.HIGHEST
    )


def local(hamiltonian, pattern, ortho, lists):
    local_count = hamiltonian.shape[0]
    block_size = hamiltonian.shape[-1]
    first = lax.axis_index(("space", "inner")) * local_count
    masked = hamiltonian * pattern[:, :, None, None].astype(jnp.bfloat16)
    global_cols = first + jnp.arange(local_count, dtype=jnp.int32)
    upper = jnp.where((global_cols == 0)[:, None, None], jnp.zeros_like(ortho[:, 0]), ortho[:, 0])
    diag_z = (jnp.eye(block_size, dtype=jnp.float32) + ortho[:, 1].astype(jnp.float32)).astype(
        jnp.bfloat16
    )
    stacked = jnp.stack([upper, diag_z], 1)
    ham_reach = -(-Q // local_count)
    ortho_reach = -(-(Q + 2) // local_count)
    ortho_pieces = []
    for offset in range(-ortho_reach, ortho_reach + 1):
        if offset == 0:
            ortho_pieces.append(stacked)
        else:
            ortho_pieces.append(shifted_2(stacked, ("space", "inner"), -offset))
    ortho_ext = jnp.concatenate(ortho_pieces, 0)
    left_piece = shifted_2(masked[-1:], ("space", "inner"), 1)
    with_left = jnp.concatenate([left_piece, masked], 0)
    strip_pieces = []
    own_orth = orth_columns(with_left, ortho_ext, 1, ortho_reach * local_count, local_count, RO)
    for offset in range(-ham_reach, ham_reach + 1):
        if offset == 0:
            strip_pieces.append(own_orth)
        else:
            strip_pieces.append(shifted_2(own_orth, ("space", "inner"), -offset))
    orth_ext = jnp.concatenate(strip_pieces, 0)
    orth_base = first - ham_reach * local_count
    bands = lax.map(
        lambda item: solve_column(orth_ext, orth_base, item[0], item[1]), (lists, global_cols)
    )
    next_piece = shifted_2(bands[:1].astype(jnp.bfloat16), ("space", "inner"), -1).astype(
        jnp.float32
    )
    following = jnp.concatenate([bands[1:], next_piece], 0)
    return back_transform(bands, following, ortho_ext, ortho_reach * local_count, local_count)


def solution(mesh):
    in_specs = (
        P(("space", "inner"), None, None, None),
        P(("space", "inner"), None),
        P(("space", "inner"), None, None, None),
        P(("space", "inner"), None),
    )
    out_specs = P(("space", "inner"), None, None, None)
    return jax.shard_map(local, mesh=mesh, in_specs=in_specs, out_specs=out_specs, check_vma=False)
```

profile of v0, /device:TPU:127, one launch (start us, length us, event | category | flops | bytes accessed | tf_op | source)
XLA Modules:
  0.0 173.5 jit_solution(5712187178007729926)
XLA Ops:
  1.8 5.3 %collective-permute-start = (bf16[2,2,128,128]{3,2,1,0:T(8,128)(2,1)S(1)}, bf16[2,2,128,128]{3,2,1,0:T(8,128)(2,1)S(1)}, u32[]{:S(2)}, u32[]{:S(2)}) collective-permute-start(bf16[2,2,128,128]{3,2,1,0:T(8,128)(2,1)S(1)} %pad_maximum_fusion.1), channel_id=1, source_target_pairs={{0,4},{1,5},{2,6},{3,7},{4,8},{5,9},{6,10},{7,11},{8,12},{9,13},{1... | collective-permute-start | bytes 393224 | tf_op jit(solution)/shard_map/ppermute | solution.py:18
  7.1 4.6 %collective-permute-start.1 = (bf16[2,2,128,128]{3,2,1,0:T(8,128)(2,1)S(1)}, bf16[2,2,128,128]{3,2,1,0:T(8,128)(2,1)S(1)}, u32[]{:S(2)}, u32[]{:S(2)}) collective-permute-start(bf16[2,2,128,128]{3,2,1,0:T(8,128)(2,1)S(1)} %pad_maximum_fusion.1), channel_id=1, source_target_pairs={{0,3},{1,4},{2,5},{3,6},{4,7},{5,8},{6,9},{7,10},{8,11},{9,12},{10... | collective-permute-start | bytes 393224 | tf_op jit(solution)/shard_map/ppermute | solution.py:18
  11.7 2.6 %collective-permute-start.2 = (bf16[2,2,128,128]{3,2,1,0:T(8,128)(2,1)S(1)}, bf16[2,2,128,128]{3,2,1,0:T(8,128)(2,1)S(1)}, u32[]{:S(2)}, u32[]{:S(2)}) collective-permute-start(bf16[2,2,128,128]{3,2,1,0:T(8,128)(2,1)S(1)} %pad_maximum_fusion.1), channel_id=1, source_target_pairs={{0,2},{1,3},{2,4},{3,5},{4,6},{5,7},{6,8},{7,9},{8,10},{9,11},{10,... | collective-permute-start | bytes 393224 | tf_op jit(solution)/shard_map/ppermute | solution.py:18
  21.8 2.7 %collective-permute-start.5 = (bf16[2,2,128,128]{3,2,1,0:T(8,128)(2,1)S(1)}, bf16[2,2,128,128]{3,2,1,0:T(8,128)(2,1)S(1)}, u32[]{:S(2)}, u32[]{:S(2)}) collective-permute-start(bf16[2,2,128,128]{3,2,1,0:T(8,128)(2,1)S(1)} %pad_maximum_fusion.1), channel_id=1, source_target_pairs={{2,0},{3,1},{4,2},{5,3},{6,4},{7,5},{8,6},{9,7},{10,8},{11,9},{12,... | collective-permute-start | bytes 393224 | tf_op jit(solution)/shard_map/ppermute | solution.py:18
  24.5 2.8 %collective-permute-start.6 = (bf16[2,2,128,128]{3,2,1,0:T(8,128)(2,1)S(1)}, bf16[2,2,128,128]{3,2,1,0:T(8,128)(2,1)S(1)}, u32[]{:S(2)}, u32[]{:S(2)}) collective-permute-start(bf16[2,2,128,128]{3,2,1,0:T(8,128)(2,1)S(1)} %pad_maximum_fusion.1), channel_id=1, source_target_pairs={{3,0},{4,1},{5,2},{6,3},{7,4},{8,5},{9,6},{10,7},{11,8},{12,9},{13... | collective-permute-start | bytes 393224 | tf_op jit(solution)/shard_map/ppermute | solution.py:18
  27.4 4.6 %collective-permute-start.7 = (bf16[2,2,128,128]{3,2,1,0:T(8,128)(2,1)S(1)}, bf16[2,2,128,128]{3,2,1,0:T(8,128)(2,1)S(1)}, u32[]{:S(2)}, u32[]{:S(2)}) collective-permute-start(bf16[2,2,128,128]{3,2,1,0:T(8,128)(2,1)S(1)} %pad_maximum_fusion.1), channel_id=1, source_target_pairs={{4,0},{5,1},{6,2},{7,3},{8,4},{9,5},{10,6},{11,7},{12,8},{13,9},{1... | collective-permute-start | bytes 393224 | tf_op jit(solution)/shard_map/ppermute | solution.py:18
  32.1 8.3 %collective-permute-start.8 = (bf16[1,5,128,128]{3,2,1,0:T(8,128)(2,1)S(1)}, bf16[1,5,128,128]{3,2,1,0:T(8,128)(2,1)S(1)}, u32[]{:S(2)}, u32[]{:S(2)}) collective-permute-start(bf16[1,5,128,128]{3,2,1,0:T(8,128)(2,1)S(1)} %slice.77), channel_id=1, source_target_pairs={{0,1},{1,2},{2,3},{3,4},{4,5},{5,6},{6,7},{7,8},{8,9},{9,10},{10,1... | collective-permute-start | bytes 491528 | tf_op jit(solution)/shard_map/ppermute | solution.py:18
  45.0 5.1 %collective-permute-start.9 = (bf16[2,4,128,128]{3,2,1,0:T(8,128)(2,1)S(1)}, bf16[2,4,128,128]{3,2,1,0:T(8,128)(2,1)S(1)}, u32[]{:S(2)}, u32[]{:S(2)}) collective-permute-start(bf16[2,4,128,128]{3,2,1,0:T(8,128)(2,1)S(1)} %fusion.64), channel_id=1, source_target_pairs={{0,3},{1,4},{2,5},{3,6},{4,7},{5,8},{6,9},{7,10},{8,11},{9,12},{10... | collective-permute-start | bytes 786440 | tf_op jit(solution)/shard_map/ppermute | solution.py:18
  50.1 4.2 %collective-permute-start.10 = (bf16[2,4,128,128]{3,2,1,0:T(8,128)(2,1)S(1)}, bf16[2,4,128,128]{3,2,1,0:T(8,128)(2,1)S(1)}, u32[]{:S(2)}, u32[]{:S(2)}) collective-permute-start(bf16[2,4,128,128]{3,2,1,0:T(8,128)(2,1)S(1)} %fusion.64), channel_id=1, source_target_pairs={{0,2},{1,3},{2,4},{3,5},{4,6},{5,7},{6,8},{7,9},{8,10},{9,11},{10,... | collective-permute-start | bytes 786440 | tf_op jit(solution)/shard_map/ppermute | solution.py:18
  54.3 4.3 %collective-permute-start.11 = (bf16[2,4,128,128]{3,2,1,0:T(8,128)(2,1)S(1)}, bf16[2,4,128,128]{3,2,1,0:T(8,128)(2,1)S(1)}, u32[]{:S(2)}, u32[]{:S(2)}) collective-permute-start(bf16[2,4,128,128]{3,2,1,0:T(8,128)(2,1)S(1)} %fusion.64), channel_id=1, source_target_pairs={{0,1},{1,2},{2,3},{3,4},{4,5},{5,6},{6,7},{7,8},{8,9},{9,10},{10,1... | collective-permute-start | bytes 786440 | tf_op jit(solution)/shard_map/ppermute | solution.py:18
  60.9 3.3 %collective-permute-start.13 = (bf16[2,4,128,128]{3,2,1,0:T(8,128)(2,1)S(1)}, bf16[2,4,128,128]{3,2,1,0:T(8,128)(2,1)S(1)}, u32[]{:S(2)}, u32[]{:S(2)}) collective-permute-start(bf16[2,4,128,128]{3,2,1,0:T(8,128)(2,1)S(1)} %fusion.64), channel_id=1, source_target_pairs={{2,0},{3,1},{4,2},{5,3},{6,4},{7,5},{8,6},{9,7},{10,8},{11,9},{12,... | collective-permute-start | bytes 786440 | tf_op jit(solution)/shard_map/ppermute | solution.py:18
  64.2 3.0 %collective-permute-start.14 = (bf16[2,4,128,128]{3,2,1,0:T(8,128)(2,1)S(1)}, bf16[2,4,128,128]{3,2,1,0:T(8,128)(2,1)S(1)}, u32[]{:S(2)}, u32[]{:S(2)}) collective-permute-start(bf16[2,4,128,128]{3,2,1,0:T(8,128)(2,1)S(1)} %fusion.64), channel_id=1, source_target_pairs={{3,0},{4,1},{5,2},{6,3},{7,4},{8,5},{9,6},{10,7},{11,8},{12,9},{13... | collective-permute-start | bytes 786440 | tf_op jit(solution)/shard_map/ppermute | solution.py:18
  70.1 2.6 %collective-permute-done.12 = bf16[2,4,128,128]{3,2,1,0:T(8,128)(2,1)S(1)} collective-permute-done((bf16[2,4,128,128]{3,2,1,0:T(8,128)(2,1)S(1)}, bf16[2,4,128,128]{3,2,1,0:T(8,128)(2,1)S(1)}, u32[]{:S(2)}, u32[]{:S(2)}) %collective-permute-start.12) | collective-permute-done | bytes 262176 | tf_op jit(solution)/shard_map/ppermute | solution.py:18
  73.5 4.0 %collective-permute-done.13 = bf16[2,4,128,128]{3,2,1,0:T(8,128)(2,1)S(1)} collective-permute-done((bf16[2,4,128,128]{3,2,1,0:T(8,128)(2,1)S(1)}, bf16[2,4,128,128]{3,2,1,0:T(8,128)(2,1)S(1)}, u32[]{:S(2)}, u32[]{:S(2)}) %collective-permute-start.13) | collective-permute-done | bytes 262176 | tf_op jit(solution)/shard_map/ppermute | solution.py:18
  81.4 69.2 %while.10 = (s32[]{:T(128)}, f32[2,11,128,128]{3,2,1,0:T(8,128)}, s32[2,6]{1,0:T(2,128)S(1)}, s32[2]{0:T(128)S(1)}, s32[]{:T(128)}, /*index=5*/bf16[14,4,128,128...) while((s32[]{:T(128)}, f32[2,11,128,128]{3,2,1,0:T(8,128)}, s32[2,6]{1,0:T(2,128)S(1)}, ...), condition=%wide.region_3.4_spmd, body=%wide.region_0.3_spmd.sunk | while | flops 3967848448 | bytes 50824256 | solution.py:157
  82.8 3.1 %gather_fusion = bf16[6,4,128,128]{3,2,1,0:T(8,128)(2,1)} fusion(bf16[14,4,128,128]{3,2,1,0:T(8,128)(2,1)} %get-tuple-element.147, s32[1024]{0:T(1024)S(1)} %pad_clamp_fusion.5), kind=kCustom, calls=%fused_computation.clone.1 | custom fusion | bytes 1572888 | tf_op jit(solution)/shard_map/while/body/eval_jaxpr/gather | solution.py:51
  87.8 2.7 %copy.95 = f32[6,128,128,6]{1,0,2,3:T(8,128)} copy(f32[6,128,128,6]{2,3,1,0:T(8,128)S(1)} %fusion.123) | data formatting | bytes 4718592 | tf_op jit(solution)/shard_map/while/body/eval_jaxpr/str,srba->satb/dot_general | solution.py:71
  90.8 4.0 %multiply_reduce_fusion.2 = (f32[]{:T(128)}, f32[6,128,6,128]{3,0,1,2:T(8,128)S(1)}) fusion(f32[6]{0:T(128)S(1)} %get-tuple-element.112, s32[6,128]{1,0:T(8,128)S(1)} %multiply_add_fusion.2, s32[6,128]{0,1:T(8,128)S(1)} %copy.94, f32[6,128,128,6]{1,0,2,3:T(8,128)} %copy.95, pred[6,6,4,1]{0,2,3,1:T(4,128)(4,1)S(1)} %copy.96, ...), kind=kOutput, calls=%fused_computation.11.clone.1 | convolution fusion | flops 8847359 | bytes 5511340 | tf_op jit(solution)/shard_map/while/body/eval_jaxpr/str,trab->satb/dot_general | solution.py:65
  99.3 3.0 %copy.97 = f32[6,128,6,128]{3,2,1,0:T(8,128)} copy(f32[6,128,6,128]{3,0,1,2:T(8,128)S(1)} %get-tuple-element.119) | data formatting | bytes 4718592 | tf_op jit(solution)/shard_map/while/body/eval_jaxpr/add | solution.py:71
  102.4 4.9 %convolution_convert_fusion.4 = bf16[768,768]{1,0:T(8,128)(2,1)S(1)} fusion(f32[96,8,6,128]{3,2,1,0:T(8,128)} %bitcast.118, f32[]{:T(128)S(6)} %mul.120, f32[768]{0:T(1024)S(1)} %broadcast_bitcast_fusion.2, bf16[96,8,6,128]{3,2,1,0:T(8,128)(2,1)} %bitcast.119), kind=kOutput, calls=%fused_computation.22.clone.1 | convolution fusion | flops 1819017216 | bytes 4721668 | tf_op jit(solution)/shard_map/while/body/eval_jaxpr/dot_general | solution.py:46
  107.3 3.0 %convolution_convert_fusion.5 = bf16[768,768]{1,0:T(8,128)(2,1)} fusion(bf16[768,768]{1,0:T(8,128)(2,1)S(1)} %convolution_convert_fusion.4), kind=kOutput, calls=%fused_computation.21.clone.1 | convolution fusion | flops 1815478272 | bytes 2359296 | tf_op jit(solution)/shard_map/while/body/eval_jaxpr/dot_general | solution.py:46
  110.5 3.1 %fusion.124 = f32[768,128]{1,0:T(8,128)S(1)} fusion(bf16[768,768]{1,0:T(8,128)(2,1)} %convolution_convert_fusion.5, pred[768,768]{1,0:T(32,128)(4,1)S(1)} %iota_compare_fusion.4), kind=kOutput, calls=%fused_computation.27.clone.1 | convolution fusion | flops 302678016 | bytes 3145728 | tf_op jit(solution)/shard_map/while/body/eval_jaxpr/dot_general | solution.py:46
  117.4 3.1 %gather_fusion = bf16[6,4,128,128]{3,2,1,0:T(8,128)(2,1)} fusion(bf16[14,4,128,128]{3,2,1,0:T(8,128)(2,1)} %get-tuple-element.147, s32[1024]{0:T(1024)S(1)} %pad_clamp_fusion.5), kind=kCustom, calls=%fused_computation.clone.1 | custom fusion | bytes 1572888 | tf_op jit(solution)/shard_map/while/body/eval_jaxpr/gather | solution.py:51
  122.4 2.7 %copy.95 = f32[6,128,128,6]{1,0,2,3:T(8,128)} copy(f32[6,128,128,6]{2,3,1,0:T(8,128)S(1)} %fusion.123) | data formatting | bytes 4718592 | tf_op jit(solution)/shard_map/while/body/eval_jaxpr/str,srba->satb/dot_general | solution.py:71
  125.4 4.0 %multiply_reduce_fusion.2 = (f32[]{:T(128)}, f32[6,128,6,128]{3,0,1,2:T(8,128)S(1)}) fusion(f32[6]{0:T(128)S(1)} %get-tuple-element.112, s32[6,128]{1,0:T(8,128)S(1)} %multiply_add_fusion.2, s32[6,128]{0,1:T(8,128)S(1)} %copy.94, f32[6,128,128,6]{1,0,2,3:T(8,128)} %copy.95, pred[6,6,4,1]{0,2,3,1:T(4,128)(4,1)S(1)} %copy.96, ...), kind=kOutput, calls=%fused_computation.11.clone.1 | convolution fusion | flops 8847359 | bytes 5511340 | tf_op jit(solution)/shard_map/while/body/eval_jaxpr/str,trab->satb/dot_general | solution.py:65
  133.9 3.0 %copy.97 = f32[6,128,6,128]{3,2,1,0:T(8,128)} copy(f32[6,128,6,128]{3,0,1,2:T(8,128)S(1)} %get-tuple-element.119) | data formatting | bytes 4718592 | tf_op jit(solution)/shard_map/while/body/eval_jaxpr/add | solution.py:71
  137.0 4.9 %convolution_convert_fusion.4 = bf16[768,768]{1,0:T(8,128)(2,1)S(1)} fusion(f32[96,8,6,128]{3,2,1,0:T(8,128)} %bitcast.118, f32[]{:T(128)S(6)} %mul.120, f32[768]{0:T(1024)S(1)} %broadcast_bitcast_fusion.2, bf16[96,8,6,128]{3,2,1,0:T(8,128)(2,1)} %bitcast.119), kind=kOutput, calls=%fused_computation.22.clone.1 | convolution fusion | flops 1819017216 | bytes 4721668 | tf_op jit(solution)/shard_map/while/body/eval_jaxpr/dot_general | solution.py:46
  141.9 3.0 %convolution_convert_fusion.5 = bf16[768,768]{1,0:T(8,128)(2,1)} fusion(bf16[768,768]{1,0:T(8,128)(2,1)S(1)} %convolution_convert_fusion.4), kind=kOutput, calls=%fused_computation.21.clone.1 | convolution fusion | flops 1815478272 | bytes 2359296 | tf_op jit(solution)/shard_map/while/body/eval_jaxpr/dot_general | solution.py:46
  145.1 3.1 %fusion.124 = f32[768,128]{1,0:T(8,128)S(1)} fusion(bf16[768,768]{1,0:T(8,128)(2,1)} %convolution_convert_fusion.5, pred[768,768]{1,0:T(32,128)(4,1)S(1)} %iota_compare_fusion.4), kind=kOutput, calls=%fused_computation.27.clone.1 | convolution fusion | flops 302678016 | bytes 3145728 | tf_op jit(solution)/shard_map/while/body/eval_jaxpr/dot_general | solution.py:46
  152.6 5.2 %collective-permute-start.15 = (bf16[1,11,128,128]{3,2,1,0:T(8,128)(2,1)}, bf16[1,11,128,128]{3,2,1,0:T(8,128)(2,1)}, u32[]{:S(2)}, u32[]{:S(2)}) collective-permute-start(bf16[1,11,128,128]{3,2,1,0:T(8,128)(2,1)} %slice.101), channel_id=1, source_target_pairs={{1,0},{2,1},{3,2},{4,3},{5,4},{6,5},{7,6},{8,7},{9,8},{10,9},{11,1... | collective-permute-start | bytes 1081352 | tf_op jit(solution)/shard_map/ppermute | solution.py:18
  157.9 2.5 %gather_fusion.7 = bf16[2,128,128]{2,1,0:T(8,128)(2,1)} fusion(bf16[18,2,128,128]{3,2,1,0:T(8,128)(2,1)} %copy-done, s32[2]{0:T(128)S(1)} %copy-done.10), kind=kCustom, calls=%fused_computation.7 | custom fusion | bytes 131088 | tf_op jit(solution)/shard_map/gather | solution.py:108
  164.2 3.1 %collective-permute-done.15 = bf16[1,11,128,128]{3,2,1,0:T(8,128)(2,1)} collective-permute-done((bf16[1,11,128,128]{3,2,1,0:T(8,128)(2,1)}, bf16[1,11,128,128]{3,2,1,0:T(8,128)(2,1)}, u32[]{:S(2)}, u32[]{:S(2)}) %collective-permute-start.15) | collective-permute-done | bytes 360480 | tf_op jit(solution)/shard_map/ppermute | solution.py:18
  (135 shorter events, 54.4 us)
Async XLA Ops:
  1.8 38.8 %copy-start.12 = (s32[2]{0:T(128)S(1)}, s32[2]{0:T(128)}, u32[]{:S(2)}) copy-start(s32[2]{0:T(128)} %constant.241) | copy-start | bytes 28
  1.8 19.9 %collective-permute-start = (bf16[2,2,128,128]{3,2,1,0:T(8,128)(2,1)S(1)}, bf16[2,2,128,128]{3,2,1,0:T(8,128)(2,1)S(1)}, u32[]{:S(2)}, u32[]{:S(2)}) collective-permute-start(bf16[2,2,128,128]{3,2,1,0:T(8,128)(2,1)S(1)} %pad_maximum_fusion.1), channel_id=1, source_target_pairs={{0,4},{1,5},{2,6},{3,7},{4,8},{5,9},{6,10},{7,11},{8,12},{9,13},{1... | collective-permute-start | bytes 393224 | tf_op jit(solution)/shard_map/ppermute | solution.py:18
  7.1 17.4 %collective-permute-start.1 = (bf16[2,2,128,128]{3,2,1,0:T(8,128)(2,1)S(1)}, bf16[2,2,128,128]{3,2,1,0:T(8,128)(2,1)S(1)}, u32[]{:S(2)}, u32[]{:S(2)}) collective-permute-start(bf16[2,2,128,128]{3,2,1,0:T(8,128)(2,1)S(1)} %pad_maximum_fusion.1), channel_id=1, source_target_pairs={{0,3},{1,4},{2,5},{3,6},{4,7},{5,8},{6,9},{7,10},{8,11},{9,12},{10... | collective-permute-start | bytes 393224 | tf_op jit(solution)/shard_map/ppermute | solution.py:18
  11.7 15.7 %collective-permute-start.2 = (bf16[2,2,128,128]{3,2,1,0:T(8,128)(2,1)S(1)}, bf16[2,2,128,128]{3,2,1,0:T(8,128)(2,1)S(1)}, u32[]{:S(2)}, u32[]{:S(2)}) collective-permute-start(bf16[2,2,128,128]{3,2,1,0:T(8,128)(2,1)S(1)} %pad_maximum_fusion.1), channel_id=1, source_target_pairs={{0,2},{1,3},{2,4},{3,5},{4,6},{5,7},{6,8},{7,9},{8,10},{9,11},{10,... | collective-permute-start | bytes 393224 | tf_op jit(solution)/shard_map/ppermute | solution.py:18
  14.3 17.8 %collective-permute-start.3 = (bf16[2,2,128,128]{3,2,1,0:T(8,128)(2,1)S(1)}, bf16[2,2,128,128]{3,2,1,0:T(8,128)(2,1)S(1)}, u32[]{:S(2)}, u32[]{:S(2)}) collective-permute-start(bf16[2,2,128,128]{3,2,1,0:T(8,128)(2,1)S(1)} %pad_maximum_fusion.1), channel_id=1, source_target_pairs={{0,1},{1,2},{2,3},{3,4},{4,5},{5,6},{6,7},{7,8},{8,9},{9,10},{10,1... | collective-permute-start | bytes 393224 | tf_op jit(solution)/shard_map/ppermute | solution.py:18
  16.2 24.2 %collective-permute-start.4 = (bf16[2,2,128,128]{3,2,1,0:T(8,128)(2,1)S(1)}, bf16[2,2,128,128]{3,2,1,0:T(8,128)(2,1)S(1)}, u32[]{:S(2)}, u32[]{:S(2)}) collective-permute-start(bf16[2,2,128,128]{3,2,1,0:T(8,128)(2,1)S(1)} %pad_maximum_fusion.1), channel_id=1, source_target_pairs={{1,0},{2,1},{3,2},{4,3},{5,4},{6,5},{7,6},{8,7},{9,8},{10,9},{11,1... | collective-permute-start | bytes 393224 | tf_op jit(solution)/shard_map/ppermute | solution.py:18
  19.3 21.9 %copy-start.11 = (s32[2]{0:T(128)S(1)}, s32[2]{0:T(128)}, u32[]{:S(2)}) copy-start(s32[2]{0:T(128)} %constant.232) | copy-start | bytes 28
  21.8 18.7 %collective-permute-start.5 = (bf16[2,2,128,128]{3,2,1,0:T(8,128)(2,1)S(1)}, bf16[2,2,128,128]{3,2,1,0:T(8,128)(2,1)S(1)}, u32[]{:S(2)}, u32[]{:S(2)}) collective-permute-start(bf16[2,2,128,128]{3,2,1,0:T(8,128)(2,1)S(1)} %pad_maximum_fusion.1), channel_id=1, source_target_pairs={{2,0},{3,1},{4,2},{5,3},{6,4},{7,5},{8,6},{9,7},{10,8},{11,9},{12,... | collective-permute-start | bytes 393224 | tf_op jit(solution)/shard_map/ppermute | solution.py:18
  24.5 16.0 %collective-permute-start.6 = (bf16[2,2,128,128]{3,2,1,0:T(8,128)(2,1)S(1)}, bf16[2,2,128,128]{3,2,1,0:T(8,128)(2,1)S(1)}, u32[]{:S(2)}, u32[]{:S(2)}) collective-permute-start(bf16[2,2,128,128]{3,2,1,0:T(8,128)(2,1)S(1)} %pad_maximum_fusion.1), channel_id=1, source_target_pairs={{3,0},{4,1},{5,2},{6,3},{7,4},{8,5},{9,6},{10,7},{11,8},{12,9},{13... | collective-permute-start | bytes 393224 | tf_op jit(solution)/shard_map/ppermute | solution.py:18
  27.4 13.2 %collective-permute-start.7 = (bf16[2,2,128,128]{3,2,1,0:T(8,128)(2,1)S(1)}, bf16[2,2,128,128]{3,2,1,0:T(8,128)(2,1)S(1)}, u32[]{:S(2)}, u32[]{:S(2)}) collective-permute-start(bf16[2,2,128,128]{3,2,1,0:T(8,128)(2,1)S(1)} %pad_maximum_fusion.1), channel_id=1, source_target_pairs={{4,0},{5,1},{6,2},{7,3},{8,4},{9,5},{10,6},{11,7},{12,8},{13,9},{1... | collective-permute-start | bytes 393224 | tf_op jit(solution)/shard_map/ppermute | solution.py:18
  32.1 10.6 %collective-permute-start.8 = (bf16[1,5,128,128]{3,2,1,0:T(8,128)(2,1)S(1)}, bf16[1,5,128,128]{3,2,1,0:T(8,128)(2,1)S(1)}, u32[]{:S(2)}, u32[]{:S(2)}) collective-permute-start(bf16[1,5,128,128]{3,2,1,0:T(8,128)(2,1)S(1)} %slice.77), channel_id=1, source_target_pairs={{0,1},{1,2},{2,3},{3,4},{4,5},{5,6},{6,7},{7,8},{8,9},{9,10},{10,1... | collective-permute-start | bytes 491528 | tf_op jit(solution)/shard_map/ppermute | solution.py:18
  40.6 2.8 %copy-start = (bf16[18,2,128,128]{3,2,1,0:T(8,128)(2,1)}, bf16[18,2,128,128]{3,2,1,0:T(8,128)(2,1)S(1)}, u32[]{:S(2)}) copy-start(bf16[18,2,128,128]{3,2,1,0:T(8,128)(2,1)S(1)} %constant_dynamic-update-slice_fusion) | copy-start | bytes 3538948
  45.0 19.2 %collective-permute-start.9 = (bf16[2,4,128,128]{3,2,1,0:T(8,128)(2,1)S(1)}, bf16[2,4,128,128]{3,2,1,0:T(8,128)(2,1)S(1)}, u32[]{:S(2)}, u32[]{:S(2)}) collective-permute-start(bf16[2,4,128,128]{3,2,1,0:T(8,128)(2,1)S(1)} %fusion.64), channel_id=1, source_target_pairs={{0,3},{1,4},{2,5},{3,6},{4,7},{5,8},{6,9},{7,10},{8,11},{9,12},{10... | collective-permute-start | bytes 786440 | tf_op jit(solution)/shard_map/ppermute | solution.py:18
  50.1 17.9 %collective-permute-start.10 = (bf16[2,4,128,128]{3,2,1,0:T(8,128)(2,1)S(1)}, bf16[2,4,128,128]{3,2,1,0:T(8,128)(2,1)S(1)}, u32[]{:S(2)}, u32[]{:S(2)}) collective-permute-start(bf16[2,4,128,128]{3,2,1,0:T(8,128)(2,1)S(1)} %fusion.64), channel_id=1, source_target_pairs={{0,2},{1,3},{2,4},{3,5},{4,6},{5,7},{6,8},{7,9},{8,10},{9,11},{10,... | collective-permute-start | bytes 786440 | tf_op jit(solution)/shard_map/ppermute | solution.py:18
  54.3 14.4 %collective-permute-start.11 = (bf16[2,4,128,128]{3,2,1,0:T(8,128)(2,1)S(1)}, bf16[2,4,128,128]{3,2,1,0:T(8,128)(2,1)S(1)}, u32[]{:S(2)}, u32[]{:S(2)}) collective-permute-start(bf16[2,4,128,128]{3,2,1,0:T(8,128)(2,1)S(1)} %fusion.64), channel_id=1, source_target_pairs={{0,1},{1,2},{2,3},{3,4},{4,5},{5,6},{6,7},{7,8},{8,9},{9,10},{10,1... | collective-permute-start | bytes 786440 | tf_op jit(solution)/shard_map/ppermute | solution.py:18
  58.6 14.2 %collective-permute-start.12 = (bf16[2,4,128,128]{3,2,1,0:T(8,128)(2,1)S(1)}, bf16[2,4,128,128]{3,2,1,0:T(8,128)(2,1)S(1)}, u32[]{:S(2)}, u32[]{:S(2)}) collective-permute-start(bf16[2,4,128,128]{3,2,1,0:T(8,128)(2,1)S(1)} %fusion.64), channel_id=1, source_target_pairs={{1,0},{2,1},{3,2},{4,3},{5,4},{6,5},{7,6},{8,7},{9,8},{10,9},{11,1... | collective-permute-start | bytes 786440 | tf_op jit(solution)/shard_map/ppermute | solution.py:18
  60.9 16.6 %collective-permute-start.13 = (bf16[2,4,128,128]{3,2,1,0:T(8,128)(2,1)S(1)}, bf16[2,4,128,128]{3,2,1,0:T(8,128)(2,1)S(1)}, u32[]{:S(2)}, u32[]{:S(2)}) collective-permute-start(bf16[2,4,128,128]{3,2,1,0:T(8,128)(2,1)S(1)} %fusion.64), channel_id=1, source_target_pairs={{2,0},{3,1},{4,2},{5,3},{6,4},{7,5},{8,6},{9,7},{10,8},{11,9},{12,... | collective-permute-start | bytes 786440 | tf_op jit(solution)/shard_map/ppermute | solution.py:18
  64.2 16.5 %collective-permute-start.14 = (bf16[2,4,128,128]{3,2,1,0:T(8,128)(2,1)S(1)}, bf16[2,4,128,128]{3,2,1,0:T(8,128)(2,1)S(1)}, u32[]{:S(2)}, u32[]{:S(2)}) collective-permute-start(bf16[2,4,128,128]{3,2,1,0:T(8,128)(2,1)S(1)} %fusion.64), channel_id=1, source_target_pairs={{3,0},{4,1},{5,2},{6,3},{7,4},{8,5},{9,6},{10,7},{11,8},{12,9},{13... | collective-permute-start | bytes 786440 | tf_op jit(solution)/shard_map/ppermute | solution.py:18
  67.9 13.4 %copy-start.9 = (s32[2,6]{1,0:T(2,128)S(1)}, s32[2,6]{1,0:T(2,128)}, u32[]{:S(2)}) copy-start(s32[2,6]{1,0:T(2,128)} %param.27) | copy-start | bytes 148
  81.4 76.5 %copy-start.10 = (s32[2]{0:T(128)S(1)}, s32[2]{0:T(128)}, u32[]{:S(2)}) copy-start(s32[2]{0:T(128)} %constant.249) | copy-start | bytes 28
  81.4 79.0 %copy-start.7 = (s32[26]{0:T(128)S(1)}, s32[26]{0:T(128)}, u32[]{:S(2)}) copy-start(s32[26]{0:T(128)} %constant.257) | copy-start | bytes 316
  110.5 4.0 %copy-start.2 = (f32[2,11,128,128]{3,2,1,0:T(8,128)S(1)}, f32[2,11,128,128]{3,2,1,0:T(8,128)}, u32[]{:S(2)}) copy-start(f32[2,11,128,128]{3,2,1,0:T(8,128)} %get-tuple-element.133) | copy-start | bytes 4325380 | tf_op jit(solution)/shard_map/while
  114.8 1.2 copy-start.3
  145.1 4.0 %copy-start.2 = (f32[2,11,128,128]{3,2,1,0:T(8,128)S(1)}, f32[2,11,128,128]{3,2,1,0:T(8,128)}, u32[]{:S(2)}) copy-start(f32[2,11,128,128]{3,2,1,0:T(8,128)} %get-tuple-element.133) | copy-start | bytes 4325380 | tf_op jit(solution)/shard_map/while
  149.4 1.2 copy-start.3
  150.6 11.9 %copy-start.1 = (bf16[18,2,128,128]{3,2,1,0:T(8,128)(2,1)S(1)}, bf16[18,2,128,128]{3,2,1,0:T(8,128)(2,1)}, u32[]{:S(2)}) copy-start(bf16[18,2,128,128]{3,2,1,0:T(8,128)(2,1)} %copy-done) | copy-start | bytes 3538948
  150.6 11.9 %copy-start.6 = (s32[26]{0:T(128)S(1)}, s32[26]{0:T(128)}, u32[]{:S(2)}) copy-start(s32[26]{0:T(128)} %constant.223) | copy-start | bytes 316
  152.6 14.7 %collective-permute-start.15 = (bf16[1,11,128,128]{3,2,1,0:T(8,128)(2,1)}, bf16[1,11,128,128]{3,2,1,0:T(8,128)(2,1)}, u32[]{:S(2)}, u32[]{:S(2)}) collective-permute-start(bf16[1,11,128,128]{3,2,1,0:T(8,128)(2,1)} %slice.101), channel_id=1, source_target_pairs={{1,0},{2,1},{3,2},{4,3},{5,4},{6,5},{7,6},{8,7},{9,8},{10,9},{11,1... | collective-permute-start | bytes 1081352 | tf_op jit(solution)/shard_map/ppermute | solution.py:18
  160.3 3.8 %copy-start.4 = (f32[2,11,128,128]{3,2,1,0:T(8,128)S(1)}, f32[2,11,128,128]{3,2,1,0:T(8,128)}, u32[]{:S(2)}) copy-start(f32[2,11,128,128]{3,2,1,0:T(8,128)} %get-tuple-element.37) | copy-start | bytes 4325380
  164.2 4.2 %copy-start.8 = (bf16[2,128,128]{2,1,0:T(8,128)(2,1)S(1)}, bf16[2,128,128]{2,1,0:T(8,128)(2,1)}, u32[]{:S(2)}) copy-start(bf16[2,128,128]{2,1,0:T(8,128)(2,1)} %gather_fusion.7) | copy-start | bytes 196612
  170.1 1.2 copy-start.5
where the time goes:
time: 175 us; the launch traced here: 174 us
  starting transfers between devices  62.7 us (36%)
  local copies, waits for them, and re-layouts  43.2 us (25%)
  matrix products  41.5 us (24%)
  waiting for transfers between devices  12.2 us (7%)
  other arithmetic  10.7 us (6%)
  loops' own time  2.72 us (2%)
    ppermute x16, starting transfers between devices, shifted_2(): return lax.ppermute(value, axis, pairs)  62.7 us
    dot_general x6, matrix products, mat_product(): return jnp.dot(left, right, preferred_element_type=jnp.float32)  22 us
    ppermute x16, waiting for transfers between devices, shifted_2(): return lax.ppermute(value, axis, pairs)  12.2 us
    dot_general x2, matrix products, solve_column(): jnp.einsum('str,trab->satb', lower_sel.astype(jnp.bfloat16), gathered, pr...  8.04 us
    gather x2, local copies, waits for them, and re-layouts, solve_column(): gathered = orth_ext[positions]  6.1 us
    add x2, local copies, waits for them, and re-layouts, solve_column(): sub_block + jnp.einsum('str,srba->satb', upper_sel.astype(jnp.bfloat16),...  6.09 us
    dot_general x2, local copies, waits for them, and re-layouts, solve_column(): jnp.einsum('str,srba->satb', upper_sel.astype(jnp.bfloat16), gathered, pr...  5.38 us
    unnamed x35, local copies, waits for them, and re-layouts  4.68 us
  transfers between devices with their start and end apart: 16, of which 4 were waited for; matrix products, arithmetic and copies ran while one was open for 9% of the time, Pallas kernels for 0%

commit v1 on v0

v1 whole, which is shorter than its diff:
```python
import functools

import jax
import jax.numpy as jnp
from jax import lax
from jax.experimental import pallas as pl
from jax.experimental.pallas import tpu as pltpu
from jax.sharding import PartitionSpec as P


AXES = ("space", "inner")
BS = 128
RO = 3
KMAX = 6
STEPS = 3
CHEM = 0.25
OWN = 2
SPAN = 14
BACK = 6
ORDER = KMAX * BS
PAY = 10 * BS + 16
FAR = 8 * BS
TILE = 256


BF = jnp.bfloat16
F32 = jnp.float32


def nn(a, b):
    return jnp.dot(a, b, preferred_element_type=F32)


def nt(a, b):
    return lax.dot_general(a, b, (((1,), (1,)), ((), ())), preferred_element_type=F32)


def rows(i, n=1):
    return slice(i * BS, (i + n) * BS)


def eye(n, m):
    r = lax.broadcasted_iota(jnp.int32, (n, m), 0)
    c = lax.broadcasted_iota(jnp.int32, (n, m), 1)
    return jnp.where(r == c, 1.0, 0.0).astype(F32)


def pack_kernel(meta, pattern, lists, ham, ortho, pay, far):
    first, core = meta[0], meta[1]
    for c in range(OWN):
        for r in range(3):
            keep = pattern[c, r + 2].astype(F32)
            block = (ham[c, r + 2].astype(F32) * keep).astype(BF)
            pay[rows(c * 3 + r), :] = block
            far[rows(c * 3 + r), :] = block
        upper = ortho[c, 0]
        if c == 0:
            upper = jnp.where(first == 0, jnp.zeros_like(upper), upper)
        pay[rows(6 + 2 * c), :] = upper
        pay[rows(7 + 2 * c), :] = ortho[c, 1]
    far[rows(6, 2), :] = pay[rows(8, 2), :]

    @pl.when(core == 0)
    def _():
        far[rows(2), :] = pay[rows(6), :]
        far[rows(4), :] = pay[rows(7), :]

    lane = lax.broadcasted_iota(jnp.int32, (16, BS), 1)
    code = jnp.zeros((16, BS), F32)
    for s in range(KMAX):
        slot = lists[0, s]
        value = jnp.where(slot >= 0, slot - first + 8, 0).astype(F32)
        code = code + jnp.where(lane == s, value, 0.0)
    pay[10 * BS : 10 * BS + 16, :] = code.astype(BF)


def main_kernel(
    meta, lists, own, pair, near_a, near_b, cross_a, cross_b, far, out,
    hl, zc, zl, gt, up, xs, ms, ys, pb, rt, slots,
):
    core, odd_chip = meta[1], meta[2]
    ident = eye(BS, BS)

    def take(k, pay, is_far=None):
        i = 2 * k + BACK
        if is_far is None:
            for c in range(OWN):
                hl[i + c] = pay[rows(3 * c, 3), :]
                put_z(i + c, pay[rows(6 + 2 * c), :], pay[rows(7 + 2 * c), :])
        elif is_far == "left":
            for c in range(OWN):
                hl[i + c] = pay[rows(3 * c, 3), :]
            put_z(i + 1, pay[rows(6), :], pay[rows(7), :])
        else:
            for c in range(OWN):
                hl[i + c] = pay[rows(3 * c, 3), :]
            put_z(i, pay[rows(2), :], pay[rows(4), :])
            put_z(i + 1, pay[rows(6), :], pay[rows(7), :])

    def put_z(i, upper, diagonal):
        diag = (ident + diagonal.astype(F32)).astype(BF)
        zc[i, :BS, :] = upper
        zc[i, BS:, :] = diag
        zl[i, :, BS:] = upper
        zl[i + 1, :, :BS] = diag

    def slots_of(pay):
        code = pay[10 * BS : 10 * BS + 16, :].astype(F32)
        lane = lax.broadcasted_iota(jnp.int32, (16, BS), 1)
        row = lax.broadcasted_iota(jnp.int32, (16, BS), 0)
        for s in range(KMAX):
            value = jnp.sum(jnp.where((lane == s) & (row == 0), code, 0.0)).astype(jnp.int32)
            slots[2 * KMAX + s] = jnp.where(value > 0, value - 8 + BACK + 2, -1)

    take(0, own)
    for c in range(OWN):
        for s in range(KMAX):
            slot = lists[c, s]
            slots[c * KMAX + s] = jnp.where(slot >= 0, slot - meta[0] + BACK, -1)

    def sides(near_l, cross_l, near_r, cross_r):
        @pl.when(core == 0)
        def _():
            take(-3, far, "left")
            take(-2, near_l)
            take(-1, cross_l)
            take(1, pair)
            take(2, near_r)
            take(3, cross_r)
            slots_of(pair)

        @pl.when(core == 1)
        def _():
            take(-3, cross_l)
            take(-2, near_l)
            take(-1, pair)
            take(1, cross_r)
            take(2, near_r)
            take(3, far, "right")
            slots_of(cross_r)

    @pl.when(odd_chip == 0)
    def _():
        sides(near_b, cross_b, near_a, cross_a)

    @pl.when(odd_chip == 1)
    def _():
        sides(near_a, cross_a, near_b, cross_b)

    for b in range(1, SPAN):
        zu_t = zc[b, :BS, :].T
        zd_t = zc[b, BS:, :].T
        left = nt(zu_t, hl[b - 1])
        right = nt(zd_t, hl[b])
        edge = nn(zd_t, hl[b - 1, rows(1), :])
        gt[b, :, rows(0)] = (left[:, rows(0)] + edge).astype(BF)
        gt[b, :, rows(1)] = (left[:, rows(1)] + right[:, rows(0)]).astype(BF)
        gt[b, :, rows(2)] = (left[:, rows(2)] + right[:, rows(1)]).astype(BF)
        gt[b, :, rows(3)] = right[:, rows(2)].astype(BF)
    for b in range(1, SPAN):
        for k in range(RO + 1):
            if b + k < SPAN:
                if k < RO:
                    block = nn(gt[b, :, rows(k, 2)], zc[b + k])
                else:
                    block = nn(gt[b, :, rows(k)], zc[b + k, :BS, :])
                up[4 * b + k] = block.astype(BF)

    pb[...] = jnp.zeros_like(pb)

    def solve(c, carry):
        where_to = [slots[c * KMAX + s] for s in range(KMAX)]
        live = [w >= 0 for w in where_to]
        count = functools.reduce(lambda a, b: a + b, [v.astype(jnp.int32) for v in live])
        squares = jnp.zeros((BS, BS), F32)

        def pair_of(s, t):
            ws, wt = where_to[s], where_to[t]
            lo, hi = jnp.minimum(ws, wt), jnp.maximum(ws, wt)
            valid = live[s] & live[t] & (hi - lo <= RO)
            index = jnp.where(valid, 4 * lo + (hi - lo), 0)
            return valid, index, ws >= wt

        for s in range(KMAX):
            block = up[jnp.where(live[s], 4 * where_to[s], 0)].astype(F32)
            entry = jnp.where(live[s], CHEM * ident - block, 0.0)
            squares = squares + entry * entry
            for t in range(s):
                valid, index, _ = pair_of(s, t)
                block = up[index].astype(F32)
                squares = squares + jnp.where(valid, 2.0 * (block * block), 0.0)
        total = jnp.sum(squares, axis=(0, 1), keepdims=True)
        width = (jnp.maximum(count, 1) * BS).astype(F32)
        scale = 2.0 * jnp.sqrt(total / width + 1e-06)
        inverse = 1.0 / scale
        for s in range(KMAX):
            block = up[jnp.where(live[s], 4 * where_to[s], 0)].astype(F32)
            entry = jnp.where(live[s], CHEM * ident - block, 0.0) * inverse
            xs[rows(s), rows(s)] = entry.astype(BF)
            for t in range(s):
                valid, index, below = pair_of(s, t)
                block = jnp.where(valid, up[index].astype(F32) * -inverse, 0.0).astype(BF)
                turned = block.T
                xs[rows(s), rows(t)] = jnp.where(below, turned, block)
                xs[rows(t), rows(s)] = jnp.where(below, block, turned)

        tiles = [slice(i * TILE, (i + 1) * TILE) for i in range(ORDER // TILE)]
        big = eye(TILE, TILE)
        src, dst = xs, ys
        for _ in range(STEPS - 1):
            for m in tiles:
                for n in tiles:
                    square = nn(src[m, :], src[:, n])
                    base = 1.5 * big if m == n else 0.0
                    ms[m, n] = (base - 0.5 * square).astype(BF)
            for m in tiles:
                for n in tiles:
                    dst[m, n] = nn(src[m, :], ms[:, n]).astype(BF)
            src, dst = dst, src
        top = eye(TILE, BS)
        for m in tiles:
            square = nn(src[m, :], src[:, :BS])
            base = 1.5 * top if m.start == 0 else 0.0
            ms[m, :BS] = (base - 0.5 * square).astype(BF)
        lanes = pl.ds(pl.multiple_of(c * BS, BS), BS)
        for i, m in enumerate(tiles):
            part = nn(src[m, :], ms[:, :BS])
            if i == 0:
                part = part + top
            part = (0.5 * part).astype(BF)
            for h in range(TILE // BS):
                s = i * (TILE // BS) + h
                row = jnp.where(live[s], where_to[s], SPAN)
                pb[pl.ds(pl.multiple_of(row * BS, BS), BS), lanes] = part[rows(h), :]
        return carry

    lax.fori_loop(0, OWN + 1, solve, 0)

    for c in range(OWN):
        rt[:, rows(c)] = nt(pb[BS : SPAN * BS, rows(c, 2)], zl[BACK + c + 1]).astype(BF)
    for i in range(SPAN):
        if i == 0:
            part = nn(zl[1, :, BS:], rt[rows(0), :])
        elif i == SPAN - 1:
            part = nn(zl[i + 1, :, :BS], rt[rows(i - 1), :])
        else:
            part = nn(zl[i + 1], rt[rows(i - 1, 2), :])
        for c in range(OWN):
            if 0 <= i - c < 13:
                out[c, i - c] = part[:, rows(c)]


def build(mesh, interpret=False):
    n = mesh.shape["space"] * mesh.shape["inner"]
    inside = lambda i: 0 <= i < n
    swap = [(i, i ^ 1) for i in range(n)]

    def chips(parity):
        pairs = []
        for i in range(n):
            chip = i >> 1
            other = chip + 1 if (chip & 1) == parity else chip - 1
            pairs.append((i, 2 * other + (i & 1)))
        return [(a, b) for a, b in pairs if inside(b)]

    cross = [(i, i + 3 if i & 1 else i - 3) for i in range(n)]
    cross = [(a, b) for a, b in cross if inside(b)]

    def send(value, pairs):
        return lax.ppermute(value, AXES, pairs)

    vmem = pl.BlockSpec(memory_space=pltpu.VMEM)
    smem = pl.BlockSpec(memory_space=pltpu.SMEM)

    def local(hamiltonian, pattern, ortho, lists):
        device = lax.axis_index(AXES).astype(jnp.int32)
        meta = jnp.stack([device * OWN, device & 1, (device >> 1) & 1, device])
        pay, far = pl.pallas_call(
            pack_kernel,
            out_shape=(
                jax.ShapeDtypeStruct((PAY, BS), BF),
                jax.ShapeDtypeStruct((FAR, BS), BF),
            ),
            in_specs=[smem, smem, smem, vmem, vmem],
            out_specs=(vmem, vmem),
            compiler_params=pltpu.CompilerParams(vmem_limit_bytes=8 << 20),
            interpret=interpret,
        )(meta, pattern, lists, hamiltonian, ortho)
        near_b = send(pay, chips(1))
        near_a = send(pay, chips(0))
        got_far = send(far, cross)
        pair = send(pay, swap)
        cross_a = send(near_a, swap)
        cross_b = send(near_b, swap)
        out = pl.pallas_call(
            main_kernel,
            out_shape=jax.ShapeDtypeStruct((OWN, 13, BS, BS), F32),
            in_specs=[smem, smem] + [vmem] * 7,
            out_specs=vmem,
            scratch_shapes=[
                pltpu.VMEM((SPAN, 3 * BS, BS), BF),
                pltpu.VMEM((SPAN, 2 * BS, BS), BF),
                pltpu.VMEM((SPAN + 1, BS, 2 * BS), BF),
                pltpu.VMEM((SPAN, BS, 4 * BS), BF),
                pltpu.VMEM((4 * SPAN, BS, BS), BF),
                pltpu.VMEM((ORDER, ORDER), BF),
                pltpu.VMEM((ORDER, ORDER), BF),
                pltpu.VMEM((ORDER, ORDER), BF),
                pltpu.VMEM(((SPAN + 1) * BS, 3 * BS), BF),
                pltpu.VMEM(((SPAN - 1) * BS, 2 * BS), BF),
                pltpu.SMEM((3 * KMAX,), jnp.int32),
            ],
            compiler_params=pltpu.CompilerParams(vmem_limit_bytes=24 << 20),
            cost_estimate=pl.CostEstimate(
                flops=12 * 10**9, bytes_accessed=4 << 20, transcendentals=0
            ),
            interpret=interpret,
        )(meta, lists, pay, pair, near_a, near_b, cross_a, cross_b, got_far)
        return out

    spec4 = P(AXES, None, None, None)
    spec2 = P(AXES, None)
    return jax.shard_map(
        local, mesh=mesh, in_specs=(spec4, spec2, spec4, spec2), out_specs=spec4, check_vma=False
    )


def solution(mesh):
    return build(mesh)
```

time: 175 us -> 56.4 us (0.32)
  starting transfers between devices: 62.7 us -> 10.1 us
  matrix products: 41.5 us -> 0 us
  local copies, waits for them, and re-layouts: 43.2 us -> 3.91 us
  Pallas kernels: 0 us -> 21.1 us
  other arithmetic: 10.7 us -> 0.08 us
  waiting for transfers between devices: 12.2 us -> 20.8 us
  loops' own time: 2.72 us -> 0 us
    ppermute x16 -> x6, starting transfers between devices: 62.7 us -> 10.1 us  [send(): return lax.ppermute(value, AXES, pairs)]
    dot_general x20 -> x0, matrix products: 41.5 us -> none  [the longest x6 22 us: mat_product(): return jnp.dot(left, right, preferred_element_type=jnp.float32)]
    pallas_call x0 -> x2, Pallas kernels: none -> 21.1 us  [the longest x1 20.5 us: local(): pl.pallas_call(main_kernel, out_shape=jax.ShapeDtypeStruct((OWN, 13, BS,...]
    gather x11 -> x0, local copies, waits for them, and re-layouts: 15.6 us -> none  [the longest x2 6.1 us: solve_column(): gathered = orth_ext[positions]]
    ppermute x16 -> x6, waiting for transfers between devices: 12.2 us -> 20.8 us  [send(): return lax.ppermute(value, AXES, pairs)]
    add x2 -> x0, local copies, waits for them, and re-layouts: 6.09 us -> none  [solve_column(): sub_block + jnp.einsum('str,srba->satb', upper_sel.astype(jnp.bfloat16),...]
    dot_general x2 -> x0, local copies, waits for them, and re-layouts: 5.38 us -> none  [solve_column(): jnp.einsum('str,srba->satb', upper_sel.astype(jnp.bfloat16), gathered, pr...]
    convert_element_type x8 -> x0, other arithmetic: 3.96 us -> none  [the longest x2 1.36 us: solve_column(): iterate = (shifted / scale).astype(jnp.bfloat16)]
  transfers between devices with their start and end apart: 16 -> 6, of which waited for: 4 -> 2; matrix products, arithmetic and copies ran while one was open for 9% -> 0% of each run, Pallas kernels for 0% -> 0%
where the time goes in v1:
time: 56.4 us; the launch traced here: 56.1 us
  Pallas kernels  21.1 us (37%)
  waiting for transfers between devices  20.8 us (37%)
  starting transfers between devices  10.1 us (18%)
  local copies, waits for them, and re-layouts  3.91 us (7%)
    ppermute x6, waiting for transfers between devices, send(): return lax.ppermute(value, AXES, pairs)  20.8 us
    pallas_call x1, Pallas kernels, local(): pl.pallas_call(main_kernel, out_shape=jax.ShapeDtypeStruct((OWN, 13, BS,...  20.5 us
    ppermute x6, starting transfers between devices, send(): return lax.ppermute(value, AXES, pairs)  10.1 us
    unnamed x10, local copies, waits for them, and re-layouts  3.91 us
  transfers between devices with their start and end apart: 6, of which 2 were waited for; matrix products, arithmetic and copies ran while one was open for 0% of the time, Pallas kernels for 0%

profile of v1, /device:TPU:127, one launch (start us, length us, event | category | flops | bytes accessed | tf_op | source)
XLA Modules:
  0.0 56.1 jit_solution(15894300842556080709)
XLA Ops:
  0.0 0.1 pad_add_fusion.meta
  0.1 0.0 copy-start
  0.1 1.0 %copy-done = bf16[2,5,128,128]{3,2,1,0:T(8,128)(2,1)S(1)} copy-done((bf16[2,5,128,128]{3,2,1,0:T(8,128)(2,1)S(1)}, bf16[2,5,128,128]{3,2,1,0:T(8,128)(2,1)}, u32[]{:S(2)}) %copy-start) | copy-done | bytes 327704
  1.1 0.0 copy-start.1
  1.1 0.9 %copy-done.1 = bf16[2,2,128,128]{3,2,1,0:T(8,128)(2,1)S(1)} copy-done((bf16[2,2,128,128]{3,2,1,0:T(8,128)(2,1)S(1)}, bf16[2,2,128,128]{3,2,1,0:T(8,128)(2,1)}, u32[]{:S(2)}) %copy-start.1) | copy-done | bytes 131096
  2.0 0.0 copy-start.2
  2.0 0.7 %copy-done.2 = s32[2,5]{1,0:T(2,128)S(1)} copy-done((s32[2,5]{1,0:T(2,128)S(1)}, s32[2,5]{1,0:T(2,128)}, u32[]{:S(2)}) %copy-start.2) | copy-done | bytes 64
  2.6 0.0 copy-start.3
  2.6 0.7 %copy-done.3 = s32[2,6]{1,0:T(2,128)S(1)} copy-done((s32[2,6]{1,0:T(2,128)S(1)}, s32[2,6]{1,0:T(2,128)}, u32[]{:S(2)}) %copy-start.3) | copy-done | bytes 72
  3.3 0.6 %shard_map.46 = (bf16[1296,128]{1,0:T(8,128)(2,1)S(1)}, bf16[1024,128]{1,0:T(8,128)(2,1)S(1)}) custom-call(s32[4]{0:T(128)S(1)} %pad_add_fusion.meta, s32[2,5]{1,0:T(2,128)S(1)} %copy-done.2, s32[2,6]{1,0:T(2,128)S(1)} %copy-done.3, bf16[2,5,128,128]{3,2,1,0:T(8,128)(2,1)S(1)} %copy-done, bf16[2,2,128,128]{3,2,1,0:T(8,128)(2,1)S(1)} %copy-done.1), custom_call_target="tpu_custom_call" | custom-call | tf_op jit(solution)/shard_map/pallas_call | solution.py:278
  4.0 4.3 %collective-permute-start.2 = (bf16[1296,128]{1,0:T(8,128)(2,1)S(1)}, bf16[1296,128]{1,0:T(8,128)(2,1)S(1)}, u32[]{:S(2)}, u32[]{:S(2)}) collective-permute-start(bf16[1296,128]{1,0:T(8,128)(2,1)S(1)} %get-tuple-element.7.own), channel_id=1, source_target_pairs={{2,4},{3,5},{4,2},{5,3},{6,8},{7,9},{8,6},{9,7},{10,12},{11,13},{1... | collective-permute-start | bytes 995336 | tf_op jit(solution)/shard_map/ppermute | solution.py:270
  8.3 0.1 collective-permute-start.1
  8.4 1.0 %collective-permute-start = (bf16[1296,128]{1,0:T(8,128)(2,1)S(1)}, bf16[1296,128]{1,0:T(8,128)(2,1)S(1)}, u32[]{:S(2)}, u32[]{:S(2)}) collective-permute-start(bf16[1296,128]{1,0:T(8,128)(2,1)S(1)} %get-tuple-element.7.own), channel_id=1, source_target_pairs={{0,1},{1,0},{2,3},{3,2},{4,5},{5,4},{6,7},{7,6},{8,9},{9,8},{10,11... | collective-permute-start | bytes 995336 | tf_op jit(solution)/shard_map/ppermute | solution.py:270
  9.4 10.5 %collective-permute-done.2.near_b = bf16[1296,128]{1,0:T(8,128)(2,1)S(1)} collective-permute-done((bf16[1296,128]{1,0:T(8,128)(2,1)S(1)}, bf16[1296,128]{1,0:T(8,128)(2,1)S(1)}, u32[]{:S(2)}, u32[]{:S(2)}) %collective-permute-start.2) | collective-permute-done | bytes 331808 | tf_op jit(solution)/shard_map/ppermute | solution.py:270
  20.0 1.5 %collective-permute-start.4 = (bf16[1296,128]{1,0:T(8,128)(2,1)S(1)}, bf16[1296,128]{1,0:T(8,128)(2,1)S(1)}, u32[]{:S(2)}, u32[]{:S(2)}) collective-permute-start(bf16[1296,128]{1,0:T(8,128)(2,1)S(1)} %collective-permute-done.2.near_b), channel_id=1, source_target_pairs={{0,1},{1,0},{2,3},{3,2},{4,5},{5,4},{6,7},{7,6},{8,9},{9,8},{10,11... | collective-permute-start | bytes 995336 | tf_op jit(solution)/shard_map/ppermute | solution.py:270
  21.5 0.0 collective-permute-done.1.near_a
  21.5 0.0 collective-permute-start.3
  21.5 3.1 %collective-permute-start.5 = (bf16[1024,128]{1,0:T(8,128)(2,1)S(1)}, bf16[1024,128]{1,0:T(8,128)(2,1)S(1)}, u32[]{:S(2)}, u32[]{:S(2)}) collective-permute-start(bf16[1024,128]{1,0:T(8,128)(2,1)S(1)} %get-tuple-element.8), channel_id=1, source_target_pairs={{1,4},{3,6},{4,1},{5,8},{6,3},{7,10},{8,5},{9,12},{10,7},{11,14},{... | collective-permute-start | bytes 786440 | tf_op jit(solution)/shard_map/ppermute | solution.py:270
  24.6 10.3 %collective-permute-done.5.far = bf16[1024,128]{1,0:T(8,128)(2,1)S(1)} collective-permute-done((bf16[1024,128]{1,0:T(8,128)(2,1)S(1)}, bf16[1024,128]{1,0:T(8,128)(2,1)S(1)}, u32[]{:S(2)}, u32[]{:S(2)}) %collective-permute-start.5) | collective-permute-done | bytes 262176 | tf_op jit(solution)/shard_map/ppermute | solution.py:270
  34.9 0.0 collective-permute-done.pair
  34.9 0.0 collective-permute-done.4.cross_b
  34.9 0.0 collective-permute-done.3.cross_a
  34.9 0.0 copy-start.4
  34.9 0.7 %copy-done.4 = s32[2,6]{1,0:T(2,128)S(1)} copy-done((s32[2,6]{1,0:T(2,128)S(1)}, s32[2,6]{1,0:T(2,128)}, u32[]{:S(2)}) %copy-start.4) | copy-done | bytes 72
  35.6 20.5 %shard_map.47 = f32[2,13,128,128]{3,2,1,0:T(8,128)} custom-call(s32[4]{0:T(128)S(1)} %pad_add_fusion.meta, s32[2,6]{1,0:T(2,128)S(1)} %copy-done.4, bf16[1296,128]{1,0:T(8,128)(2,1)S(1)} %get-tuple-element.7.own, bf16[1296,128]{1,0:T(8,128)(2,1)S(1)} %collective-permute-done.pair, bf16[1296,128]{1,0:T(8,128)(2,1)S(1)} %collective-permute-done.1.near_a, ...), custom_call_target="tpu_custom_call" | custom-call | flops 12000000000 | bytes 4194304 | tf_op jit(solution)/shard_map/pallas_call | solution.py:295
Async XLA Ops:
  0.1 1.0 %copy-start = (bf16[2,5,128,128]{3,2,1,0:T(8,128)(2,1)S(1)}, bf16[2,5,128,128]{3,2,1,0:T(8,128)(2,1)}, u32[]{:S(2)}) copy-start(bf16[2,5,128,128]{3,2,1,0:T(8,128)(2,1)} %ham.1) | copy-start | bytes 983044
  1.1 0.9 %copy-start.1 = (bf16[2,2,128,128]{3,2,1,0:T(8,128)(2,1)S(1)}, bf16[2,2,128,128]{3,2,1,0:T(8,128)(2,1)}, u32[]{:S(2)}) copy-start(bf16[2,2,128,128]{3,2,1,0:T(8,128)(2,1)} %ortho.1) | copy-start | bytes 393220
  2.0 0.7 %copy-start.2 = (s32[2,5]{1,0:T(2,128)S(1)}, s32[2,5]{1,0:T(2,128)}, u32[]{:S(2)}) copy-start(s32[2,5]{1,0:T(2,128)} %pattern.1) | copy-start | bytes 124
  2.6 0.7 %copy-start.3 = (s32[2,6]{1,0:T(2,128)S(1)}, s32[2,6]{1,0:T(2,128)}, u32[]{:S(2)}) copy-start(s32[2,6]{1,0:T(2,128)} %lists.3) | copy-start | bytes 148
  4.0 16.0 %collective-permute-start.2 = (bf16[1296,128]{1,0:T(8,128)(2,1)S(1)}, bf16[1296,128]{1,0:T(8,128)(2,1)S(1)}, u32[]{:S(2)}, u32[]{:S(2)}) collective-permute-start(bf16[1296,128]{1,0:T(8,128)(2,1)S(1)} %get-tuple-element.7.own), channel_id=1, source_target_pairs={{2,4},{3,5},{4,2},{5,3},{6,8},{7,9},{8,6},{9,7},{10,12},{11,13},{1... | collective-permute-start | bytes 995336 | tf_op jit(solution)/shard_map/ppermute | solution.py:270
  8.3 13.2 %collective-permute-start.1 = (bf16[1296,128]{1,0:T(8,128)(2,1)S(1)}, bf16[1296,128]{1,0:T(8,128)(2,1)S(1)}, u32[]{:S(2)}, u32[]{:S(2)}) collective-permute-start(bf16[1296,128]{1,0:T(8,128)(2,1)S(1)} %get-tuple-element.7.own), channel_id=1, source_target_pairs={{0,2},{1,3},{2,0},{3,1},{4,6},{5,7},{6,4},{7,5},{8,10},{9,11},{10,... | collective-permute-start | bytes 995336 | tf_op jit(solution)/shard_map/ppermute | solution.py:270
  8.4 26.5 %collective-permute-start = (bf16[1296,128]{1,0:T(8,128)(2,1)S(1)}, bf16[1296,128]{1,0:T(8,128)(2,1)S(1)}, u32[]{:S(2)}, u32[]{:S(2)}) collective-permute-start(bf16[1296,128]{1,0:T(8,128)(2,1)S(1)} %get-tuple-element.7.own), channel_id=1, source_target_pairs={{0,1},{1,0},{2,3},{3,2},{4,5},{5,4},{6,7},{7,6},{8,9},{9,8},{10,11... | collective-permute-start | bytes 995336 | tf_op jit(solution)/shard_map/ppermute | solution.py:270
  20.0 15.0 %collective-permute-start.4 = (bf16[1296,128]{1,0:T(8,128)(2,1)S(1)}, bf16[1296,128]{1,0:T(8,128)(2,1)S(1)}, u32[]{:S(2)}, u32[]{:S(2)}) collective-permute-start(bf16[1296,128]{1,0:T(8,128)(2,1)S(1)} %collective-permute-done.2.near_b), channel_id=1, source_target_pairs={{0,1},{1,0},{2,3},{3,2},{4,5},{5,4},{6,7},{7,6},{8,9},{9,8},{10,11... | collective-permute-start | bytes 995336 | tf_op jit(solution)/shard_map/ppermute | solution.py:270
  21.5 13.4 %collective-permute-start.3 = (bf16[1296,128]{1,0:T(8,128)(2,1)S(1)}, bf16[1296,128]{1,0:T(8,128)(2,1)S(1)}, u32[]{:S(2)}, u32[]{:S(2)}) collective-permute-start(bf16[1296,128]{1,0:T(8,128)(2,1)S(1)} %collective-permute-done.1.near_a), channel_id=1, source_target_pairs={{0,1},{1,0},{2,3},{3,2},{4,5},{5,4},{6,7},{7,6},{8,9},{9,8},{10,11... | collective-permute-start | bytes 995336 | tf_op jit(solution)/shard_map/ppermute | solution.py:270
  21.5 13.4 %collective-permute-start.5 = (bf16[1024,128]{1,0:T(8,128)(2,1)S(1)}, bf16[1024,128]{1,0:T(8,128)(2,1)S(1)}, u32[]{:S(2)}, u32[]{:S(2)}) collective-permute-start(bf16[1024,128]{1,0:T(8,128)(2,1)S(1)} %get-tuple-element.8), channel_id=1, source_target_pairs={{1,4},{3,6},{4,1},{5,8},{6,3},{7,10},{8,5},{9,12},{10,7},{11,14},{... | collective-permute-start | bytes 786440 | tf_op jit(solution)/shard_map/ppermute | solution.py:270
  34.9 0.7 %copy-start.4 = (s32[2,6]{1,0:T(2,128)S(1)}, s32[2,6]{1,0:T(2,128)}, u32[]{:S(2)}) copy-start(s32[2,6]{1,0:T(2,128)} %lists.3) | copy-start | bytes 148

commit v2 on v1

v2 whole, which is shorter than its diff:
```python
import functools

import jax
import jax.numpy as jnp
from jax import lax
from jax.experimental import pallas as pl
from jax.experimental.pallas import tpu as pltpu
from jax.sharding import PartitionSpec as P


AXES = ("space", "inner")
BS = 128
RO = 3
KMAX = 6
STEPS = 3
CHEM = 0.25
OWN = 2
SPAN = 14
BACK = 6
ORDER = KMAX * BS
PAY = 9 * BS + 16
FAR = 7 * BS + 16
LISTS = 9
TILE = 256


BF = jnp.bfloat16
F32 = jnp.float32


def nn(a, b):
    return jnp.dot(a, b, preferred_element_type=F32)


def nt(a, b):
    return lax.dot_general(a, b, (((1,), (1,)), ((), ())), preferred_element_type=F32)


def rows(i, n=1):
    return slice(i * BS, (i + n) * BS)


def eye(n, m):
    r = lax.broadcasted_iota(jnp.int32, (n, m), 0)
    c = lax.broadcasted_iota(jnp.int32, (n, m), 1)
    return jnp.where(r == c, 1.0, 0.0).astype(F32)


def pack_kernel(meta, ham, ortho, pay, far, hs, os, sems):
    first, core = meta[0], meta[1]
    copies = [
        pltpu.make_async_copy(ham.at[c, pl.ds(2, 3)], hs.at[c], sems.at[c]) for c in range(OWN)
    ] + [pltpu.make_async_copy(ortho, os, sems.at[OWN])]
    for copy in copies:
        copy.start()
    for copy in copies:
        copy.wait()

    r = lax.broadcasted_iota(jnp.int32, (BS, BS), 0)
    c = lax.broadcasted_iota(jnp.int32, (BS, BS), 1)
    masked = [
        [hs[j, k].astype(F32) * meta[3 + 3 * j + k].astype(F32) for k in range(3)]
        for j in range(OWN)
    ]
    pay[rows(0), :] = jnp.where(r >= c, masked[0][0], masked[1][0]).astype(BF)
    for j in range(OWN):
        for k in range(1, 3):
            pay[rows(2 * j + k), :] = masked[j][k].astype(BF)
    pay[rows(5), :] = os[1, 0]
    pay[rows(6), :] = os[1, 1]
    pay[rows(7), :] = (os[0, 0].astype(F32) * jnp.where(first == 0, 0.0, 1.0)).astype(BF)
    pay[rows(8), :] = os[0, 1]
    diagonal = jnp.sum(jnp.where(r == c, masked[1][0], 0.0), axis=0, keepdims=True)
    lane = lax.broadcasted_iota(jnp.int32, (16, BS), 1)
    row = lax.broadcasted_iota(jnp.int32, (16, BS), 0)
    extra = jnp.where(row == 1, diagonal, 0.0)
    for s in range(KMAX):
        slot = meta[LISTS + s]
        value = jnp.where(slot >= 0, slot + 2, 0).astype(F32)
        extra = extra + jnp.where((lane == s) & (row == 0), value, 0.0)
    pay[PAY - 16 : PAY, :] = extra.astype(BF)

    far[rows(0, 7), :] = pay[rows(0, 7), :]
    far[FAR - 16 : FAR, :] = extra.astype(BF)

    @pl.when(core == 0)
    def _():
        far[rows(2, 2), :] = pay[rows(7, 2), :]


def main_kernel(
    meta, own, pair, near_a, near_b, cross_a, cross_b, far, out,
    hl, zc, zl, gt, up, xs, ms, ys, pb, rt, ob, slots, sems,
):
    core, odd_chip = meta[1], meta[2]
    r = lax.broadcasted_iota(jnp.int32, (BS, BS), 0)
    c = lax.broadcasted_iota(jnp.int32, (BS, BS), 1)
    ident = eye(BS, BS)

    def put_z(i, upper, diagonal):
        diag = (ident + diagonal.astype(F32)).astype(BF)
        zc[i, :BS, :] = upper
        zc[i, BS:, :] = diag
        zl[i, :, BS:] = upper
        zl[i + 1, :, :BS] = diag

    def take(k, pay, from_far=None):
        i = 2 * k + BACK
        size = PAY if from_far is None else FAR
        both = pay[rows(0), :].astype(F32)
        turned = pay[rows(0), :].T.astype(F32)
        last = pay[size - 16 : size, :].astype(F32)[1:2, :]
        hl[i, rows(0), :] = jnp.where(r >= c, both, turned).astype(BF)
        hl[i + 1, rows(0), :] = jnp.where(
            r < c, both, jnp.where(r > c, turned, jnp.broadcast_to(last, (BS, BS)))
        ).astype(BF)
        hl[i, rows(1, 2), :] = pay[rows(1, 2), :]
        hl[i + 1, rows(1, 2), :] = pay[rows(3, 2), :]
        put_z(i + 1, pay[rows(5), :], pay[rows(6), :])
        if from_far is None:
            put_z(i, pay[rows(7), :], pay[rows(8), :])
        elif from_far == "right":
            put_z(i, pay[rows(2), :], pay[rows(3), :])

    def slots_of(pay):
        code = pay[PAY - 16 : PAY, :].astype(F32)
        lane = lax.broadcasted_iota(jnp.int32, (16, BS), 1)
        row = lax.broadcasted_iota(jnp.int32, (16, BS), 0)
        for s in range(KMAX):
            value = jnp.sum(jnp.where((lane == s) & (row == 0), code, 0.0)).astype(jnp.int32)
            slots[2 * KMAX + s] = jnp.where(value > 0, value, -1)

    take(0, own)
    for s in range(OWN * KMAX):
        slots[s] = meta[LISTS + s]

    def sides(near_l, cross_l, near_r, cross_r):
        @pl.when(core == 0)
        def _():
            take(-3, far, "left")
            take(-2, near_l)
            take(-1, cross_l)
            take(1, pair)
            take(2, near_r)
            take(3, cross_r)
            slots_of(pair)

        @pl.when(core == 1)
        def _():
            take(-3, cross_l)
            take(-2, near_l)
            take(-1, pair)
            take(1, cross_r)
            take(2, near_r)
            take(3, far, "right")
            slots_of(cross_r)

    @pl.when(odd_chip == 0)
    def _():
        sides(near_b, cross_b, near_a, cross_a)

    @pl.when(odd_chip == 1)
    def _():
        sides(near_a, cross_a, near_b, cross_b)

    for b in range(1, SPAN):
        zu_t = zc[b, :BS, :].T
        zd_t = zc[b, BS:, :].T
        left = nt(zu_t, hl[b - 1])
        right = nt(zd_t, hl[b])
        edge = nn(zd_t, hl[b - 1, rows(1), :])
        gt[b, :, rows(0)] = (left[:, rows(0)] + edge).astype(BF)
        gt[b, :, rows(1)] = (left[:, rows(1)] + right[:, rows(0)]).astype(BF)
        gt[b, :, rows(2)] = (left[:, rows(2)] + right[:, rows(1)]).astype(BF)
        gt[b, :, rows(3)] = right[:, rows(2)].astype(BF)
    for b in range(1, SPAN):
        for k in range(RO + 1):
            if b + k < SPAN:
                if k < RO:
                    block = nn(gt[b, :, rows(k, 2)], zc[b + k])
                else:
                    block = nn(gt[b, :, rows(k)], zc[b + k, :BS, :])
                up[4 * b + k] = (-block).astype(BF)

    pb[...] = jnp.zeros_like(pb)

    def solve(c, carry):
        where_to = [slots[c * KMAX + s] for s in range(KMAX)]
        live = [w >= 0 for w in where_to]
        count = functools.reduce(lambda a, b: a + b, [v.astype(jnp.int32) for v in live])
        squares = jnp.zeros((BS, BS), F32)
        for s in range(KMAX):
            block = up[jnp.where(live[s], 4 * where_to[s], 0)].astype(F32)
            entry = jnp.where(live[s], CHEM * ident + block, 0.0)
            squares = squares + entry * entry
            xs[rows(s), rows(s)] = entry.astype(BF)
            for t in range(s):
                ws, wt = where_to[s], where_to[t]
                lo, hi = jnp.minimum(ws, wt), jnp.maximum(ws, wt)
                valid = live[s] & live[t] & (hi - lo <= RO)
                block = up[jnp.where(valid, 4 * lo + (hi - lo), 0)]
                turned = block.T
                block = jnp.where(valid, block, jnp.zeros_like(block))
                turned = jnp.where(valid, turned, jnp.zeros_like(turned))
                xs[rows(s), rows(t)] = jnp.where(ws >= wt, turned, block)
                xs[rows(t), rows(s)] = jnp.where(ws >= wt, block, turned)
                wide = block.astype(F32)
                squares = squares + 2.0 * (wide * wide)
        total = jnp.sum(squares, axis=(0, 1), keepdims=True)
        width = (jnp.maximum(count, 1) * BS).astype(F32)
        inverse = 1.0 / (2.0 * jnp.sqrt(total / width + 1e-06))
        half = 0.5 * inverse * inverse

        tiles = [slice(i * TILE, (i + 1) * TILE) for i in range(ORDER // TILE)]
        big = eye(TILE, TILE)
        src, dst = xs, ys
        for step in range(STEPS - 1):
            for i, m in enumerate(tiles):
                for n in tiles[: i + 1]:
                    square = nn(src[m, :], src[:, n])
                    base = 1.5 * big if m == n else 0.0
                    ms[m, n] = (base - (half if step == 0 else 0.5) * square).astype(BF)
            for i, m in enumerate(tiles):
                for n in tiles[: i + 1]:
                    value = nn(src[m, n.start :], ms[n.start :, n])
                    if n.start:
                        value = value + nt(src[m, : n.start], ms[n, : n.start])
                    if step == 0:
                        value = value * inverse
                    value = value.astype(BF)
                    dst[m, n] = value
                    if m != n:
                        dst[n, m] = value.T
            src, dst = dst, src
        top = eye(TILE, BS)
        for m in tiles:
            square = nn(src[m, :], src[:, :BS])
            base = 1.5 * top if m.start == 0 else 0.0
            ms[m, :BS] = (base - 0.5 * square).astype(BF)
        lanes = pl.ds(pl.multiple_of(c * BS, BS), BS)
        for i, m in enumerate(tiles):
            part = nn(src[m, :], ms[:, :BS])
            if i == 0:
                part = part + top
            part = (0.5 * part).astype(BF)
            for h in range(TILE // BS):
                s = i * (TILE // BS) + h
                row = jnp.where(live[s], where_to[s], SPAN)
                pb[pl.ds(pl.multiple_of(row * BS, BS), BS), lanes] = part[rows(h), :]
        return carry

    lax.fori_loop(0, OWN + 1, solve, 0)

    for j in range(OWN):
        rt[:, rows(j)] = nt(pb[BS : SPAN * BS, rows(j, 2)], zl[BACK + j + 1]).astype(BF)
    copies = []
    for i in range(SPAN):
        if i == 0:
            part = nn(zl[1, :, BS:], rt[rows(0), :])
        elif i == SPAN - 1:
            part = nn(zl[i + 1, :, :BS], rt[rows(i - 1), :])
        else:
            part = nn(zl[i + 1], rt[rows(i - 1, 2), :])
        for j in range(OWN):
            if 0 <= i - j < 13:
                ob[j, i - j] = part[:, rows(j)]
                copy = pltpu.make_async_copy(
                    ob.at[j, i - j], out.at[j, i - j], sems.at[j * 13 + i - j]
                )
                copy.start()
                copies.append(copy)
    for copy in copies:
        copy.wait()


def scratch():
    return [
        pltpu.VMEM((SPAN, 3 * BS, BS), BF),
        pltpu.VMEM((SPAN, 2 * BS, BS), BF),
        pltpu.VMEM((SPAN + 1, BS, 2 * BS), BF),
        pltpu.VMEM((SPAN, BS, 4 * BS), BF),
        pltpu.VMEM((4 * SPAN, BS, BS), BF),
        pltpu.VMEM((ORDER, ORDER), BF),
        pltpu.VMEM((ORDER, ORDER), BF),
        pltpu.VMEM((ORDER, ORDER), BF),
        pltpu.VMEM(((SPAN + 1) * BS, 3 * BS), BF),
        pltpu.VMEM(((SPAN - 1) * BS, 2 * BS), BF),
        pltpu.VMEM((OWN, 13, BS, BS), F32),
        pltpu.SMEM((3 * KMAX,), jnp.int32),
        pltpu.SemaphoreType.DMA((OWN * 13,)),
    ]


def build(mesh, interpret=False):
    n = mesh.shape["space"] * mesh.shape["inner"]
    inside = lambda i: 0 <= i < n
    swap = [(i, i ^ 1) for i in range(n)]

    def chips(parity):
        pairs = []
        for i in range(n):
            chip = i >> 1
            other = chip + 1 if (chip & 1) == parity else chip - 1
            pairs.append((i, 2 * other + (i & 1)))
        return [(a, b) for a, b in pairs if inside(b)]

    cross = [(i, i + 3 if i & 1 else i - 3) for i in range(n)]
    cross = [(a, b) for a, b in cross if inside(b)]

    def send(value, pairs):
        return lax.ppermute(value, AXES, pairs)

    in_hbm = lambda x: x if interpret else pltpu.with_memory_space_constraint(x, pltpu.HBM)
    vmem = pl.BlockSpec(memory_space=pltpu.VMEM)
    smem = pl.BlockSpec(memory_space=pltpu.SMEM)
    anywhere = pl.BlockSpec(memory_space=pltpu.HBM)

    def local(hamiltonian, pattern, ortho, lists):
        device = lax.axis_index(AXES).astype(jnp.int32)
        first = device * OWN
        meta = jnp.concatenate(
            [
                jnp.stack([first, device & 1, (device >> 1) & 1]),
                pattern[:, 2:].reshape(-1),
                jnp.where(lists >= 0, lists - first + BACK, -1).reshape(-1),
            ]
        )
        pay, far = pl.pallas_call(
            pack_kernel,
            out_shape=(jax.ShapeDtypeStruct((PAY, BS), BF), jax.ShapeDtypeStruct((FAR, BS), BF)),
            in_specs=[smem, anywhere, anywhere],
            out_specs=(vmem, vmem),
            scratch_shapes=[
                pltpu.VMEM((OWN, 3, BS, BS), BF),
                pltpu.VMEM((OWN, 2, BS, BS), BF),
                pltpu.SemaphoreType.DMA((OWN + 1,)),
            ],
            compiler_params=pltpu.CompilerParams(vmem_limit_bytes=8 << 20),
            interpret=interpret,
        )(meta, in_hbm(hamiltonian), in_hbm(ortho))
        near_b = send(pay, chips(1))
        near_a = send(pay, chips(0))
        got_far = send(far, cross)
        pair = send(pay, swap)
        cross_a = send(near_a, swap)
        cross_b = send(near_b, swap)
        out = pl.pallas_call(
            main_kernel,
            out_shape=jax.ShapeDtypeStruct((OWN, 13, BS, BS), F32),
            in_specs=[smem] + [vmem] * 7,
            out_specs=anywhere,
            scratch_shapes=scratch(),
            compiler_params=pltpu.CompilerParams(vmem_limit_bytes=24 << 20),
            cost_estimate=pl.CostEstimate(
                flops=12 * 10**9, bytes_accessed=4 << 20, transcendentals=0
            ),
            interpret=interpret,
        )(meta, pay, pair, near_a, near_b, cross_a, cross_b, got_far)
        return out

    spec4 = P(AXES, None, None, None)
    spec2 = P(AXES, None)
    return jax.shard_map(
        local, mesh=mesh, in_specs=(spec4, spec2, spec4, spec2), out_specs=spec4, check_vma=False
    )


def solution(mesh):
    return build(mesh)
```

time: 56.4 us -> 49.7 us (0.88)
  Pallas kernels: 21.1 us -> 17.8 us
  local copies, waits for them, and re-layouts: 3.91 us -> 0.99 us
  waiting for transfers between devices: 20.8 us -> 19.8 us
  other arithmetic: 0.08 us -> 0.68 us
    pallas_call x1, Pallas kernels: 20.5 us -> 16.1 us  [local(): pl.pallas_call(main_kernel, out_shape=jax.ShapeDtypeStruct((OWN, 13, BS,...]
    unnamed x10 -> x0, local copies, waits for them, and re-layouts: 3.91 us -> none
    pallas_call x1, Pallas kernels: 0.63 us -> 1.67 us  [local(): pl.pallas_call(pack_kernel, out_shape=(jax.ShapeDtypeStruct((PAY, BS), BF...]
    ppermute x6, waiting for transfers between devices: 20.8 us -> 19.8 us  [send(): return lax.ppermute(value, AXES, pairs)]
    slice x0 -> x1, local copies, waits for them, and re-layouts: none -> 0.75 us  [local(): pattern[:, 2:].reshape(-1)]
    select_n x0 -> x1, other arithmetic: none -> 0.68 us  [local(): jnp.where(lists >= 0, lists - first + BACK, -1).reshape(-1)]
where the time goes in v2:
time: 49.7 us; the launch traced here: 49.5 us
  waiting for transfers between devices  19.8 us (40%)
  Pallas kernels  17.8 us (36%)
  starting transfers between devices  10.1 us (20%)
  local copies, waits for them, and re-layouts  0.99 us (2%)
  other arithmetic  0.68 us (1%)
    ppermute x6, waiting for transfers between devices, send(): return lax.ppermute(value, AXES, pairs)  19.8 us
    pallas_call x1, Pallas kernels, local(): pl.pallas_call(main_kernel, out_shape=jax.ShapeDtypeStruct((OWN, 13, BS,...  16.1 us
    ppermute x6, starting transfers between devices, send(): return lax.ppermute(value, AXES, pairs)  10.1 us
    pallas_call x1, Pallas kernels, local(): pl.pallas_call(pack_kernel, out_shape=(jax.ShapeDtypeStruct((PAY, BS), BF...  1.67 us
  transfers between devices with their start and end apart: 6, of which 2 were waited for; matrix products, arithmetic and copies ran while one was open for 0% of the time, Pallas kernels for 0%

profile of v2, /device:TPU:127, one launch (start us, length us, event | category | flops | bytes accessed | tf_op | source)
XLA Modules:
  0.0 49.5 jit_solution(12319251349099368482)
XLA Ops:
  0.0 0.7 %slice.3 = s32[2,3]{1,0:T(2,128)S(1)} slice(s32[2,5]{1,0:T(2,128)} %param.5), slice={[0:2], [2:5]} | slice | bytes 48 | tf_op jit(solution)/shard_map/slice | solution.py:324
  0.8 0.1 reshape.6
  0.8 0.7 %compare_select_fusion = s32[2,6]{1,0:T(2,128)S(1)} fusion(s32[2,6]{1,0:T(2,128)} %param.7, s32[]{:T(128)} %mul.7), kind=kLoop, calls=%fused_computation | loop fusion | flops 48 | bytes 100 | tf_op jit(solution)/shard_map/jit(_where)/select_n | solution.py:325
  1.5 0.1 reshape.7
  1.6 0.1 concatenate.3.meta
  1.7 1.7 %shard_map.46 = (bf16[1168,128]{1,0:T(8,128)(2,1)S(1)}, bf16[912,128]{1,0:T(8,128)(2,1)S(1)}) custom-call(s32[21]{0:T(128)S(1)} %concatenate.3.meta, bf16[2,5,128,128]{3,2,1,0:T(8,128)(2,1)} %ham.1, bf16[2,2,128,128]{3,2,1,0:T(8,128)(2,1)} %ortho.1), custom_call_target="tpu_custom_call" | custom-call | tf_op jit(solution)/shard_map/pallas_call | solution.py:328
  3.4 4.3 %collective-permute-start.2 = (bf16[1168,128]{1,0:T(8,128)(2,1)S(1)}, bf16[1168,128]{1,0:T(8,128)(2,1)S(1)}, u32[]{:S(2)}, u32[]{:S(2)}) collective-permute-start(bf16[1168,128]{1,0:T(8,128)(2,1)S(1)} %get-tuple-element.7.own), channel_id=1, source_target_pairs={{2,4},{3,5},{4,2},{5,3},{6,8},{7,9},{8,6},{9,7},{10,12},{11,13},{1... | collective-permute-start | bytes 897032 | tf_op jit(solution)/shard_map/ppermute | solution.py:311
  7.7 0.1 collective-permute-start.1
  7.8 1.0 %collective-permute-start = (bf16[1168,128]{1,0:T(8,128)(2,1)S(1)}, bf16[1168,128]{1,0:T(8,128)(2,1)S(1)}, u32[]{:S(2)}, u32[]{:S(2)}) collective-permute-start(bf16[1168,128]{1,0:T(8,128)(2,1)S(1)} %get-tuple-element.7.own), channel_id=1, source_target_pairs={{0,1},{1,0},{2,3},{3,2},{4,5},{5,4},{6,7},{7,6},{8,9},{9,8},{10,11... | collective-permute-start | bytes 897032 | tf_op jit(solution)/shard_map/ppermute | solution.py:311
  8.8 9.8 %collective-permute-done.2.near_b = bf16[1168,128]{1,0:T(8,128)(2,1)S(1)} collective-permute-done((bf16[1168,128]{1,0:T(8,128)(2,1)S(1)}, bf16[1168,128]{1,0:T(8,128)(2,1)S(1)}, u32[]{:S(2)}, u32[]{:S(2)}) %collective-permute-start.2) | collective-permute-done | bytes 299040 | tf_op jit(solution)/shard_map/ppermute | solution.py:311
  18.7 1.5 %collective-permute-start.4 = (bf16[1168,128]{1,0:T(8,128)(2,1)S(1)}, bf16[1168,128]{1,0:T(8,128)(2,1)S(1)}, u32[]{:S(2)}, u32[]{:S(2)}) collective-permute-start(bf16[1168,128]{1,0:T(8,128)(2,1)S(1)} %collective-permute-done.2.near_b), channel_id=1, source_target_pairs={{0,1},{1,0},{2,3},{3,2},{4,5},{5,4},{6,7},{7,6},{8,9},{9,8},{10,11... | collective-permute-start | bytes 897032 | tf_op jit(solution)/shard_map/ppermute | solution.py:311
  20.2 0.0 collective-permute-done.1.near_a
  20.2 0.0 collective-permute-start.3
  20.2 3.1 %collective-permute-start.5 = (bf16[912,128]{1,0:T(8,128)(2,1)S(1)}, bf16[912,128]{1,0:T(8,128)(2,1)S(1)}, u32[]{:S(2)}, u32[]{:S(2)}) collective-permute-start(bf16[912,128]{1,0:T(8,128)(2,1)S(1)} %get-tuple-element.8), channel_id=1, source_target_pairs={{1,4},{3,6},{4,1},{5,8},{6,3},{7,10},{8,5},{9,12},{10,7},{11,14},{... | collective-permute-start | bytes 700424 | tf_op jit(solution)/shard_map/ppermute | solution.py:311
  23.3 10.0 %collective-permute-done.5.far = bf16[912,128]{1,0:T(8,128)(2,1)S(1)} collective-permute-done((bf16[912,128]{1,0:T(8,128)(2,1)S(1)}, bf16[912,128]{1,0:T(8,128)(2,1)S(1)}, u32[]{:S(2)}, u32[]{:S(2)}) %collective-permute-start.5) | collective-permute-done | bytes 233504 | tf_op jit(solution)/shard_map/ppermute | solution.py:311
  33.3 0.0 collective-permute-done.pair
  33.3 0.0 collective-permute-done.4.cross_b
  33.3 0.0 collective-permute-done.3.cross_a
  33.3 16.1 %shard_map.47 = f32[2,13,128,128]{3,2,1,0:T(8,128)} custom-call(s32[21]{0:T(128)S(1)} %concatenate.3.meta, bf16[1168,128]{1,0:T(8,128)(2,1)S(1)} %get-tuple-element.7.own, bf16[1168,128]{1,0:T(8,128)(2,1)S(1)} %collective-permute-done.pair, bf16[1168,128]{1,0:T(8,128)(2,1)S(1)} %collective-permute-done.1.near_a, ...), custom_call_target="tpu_custom_call" | custom-call | flops 12000000000 | bytes 4194304 | tf_op jit(solution)/shard_map/pallas_call | solution.py:347
Async XLA Ops:
  3.4 15.3 %collective-permute-start.2 = (bf16[1168,128]{1,0:T(8,128)(2,1)S(1)}, bf16[1168,128]{1,0:T(8,128)(2,1)S(1)}, u32[]{:S(2)}, u32[]{:S(2)}) collective-permute-start(bf16[1168,128]{1,0:T(8,128)(2,1)S(1)} %get-tuple-element.7.own), channel_id=1, source_target_pairs={{2,4},{3,5},{4,2},{5,3},{6,8},{7,9},{8,6},{9,7},{10,12},{11,13},{1... | collective-permute-start | bytes 897032 | tf_op jit(solution)/shard_map/ppermute | solution.py:311
  7.7 12.5 %collective-permute-start.1 = (bf16[1168,128]{1,0:T(8,128)(2,1)S(1)}, bf16[1168,128]{1,0:T(8,128)(2,1)S(1)}, u32[]{:S(2)}, u32[]{:S(2)}) collective-permute-start(bf16[1168,128]{1,0:T(8,128)(2,1)S(1)} %get-tuple-element.7.own), channel_id=1, source_target_pairs={{0,2},{1,3},{2,0},{3,1},{4,6},{5,7},{6,4},{7,5},{8,10},{9,11},{10,... | collective-permute-start | bytes 897032 | tf_op jit(solution)/shard_map/ppermute | solution.py:311
  7.8 25.5 %collective-permute-start = (bf16[1168,128]{1,0:T(8,128)(2,1)S(1)}, bf16[1168,128]{1,0:T(8,128)(2,1)S(1)}, u32[]{:S(2)}, u32[]{:S(2)}) collective-permute-start(bf16[1168,128]{1,0:T(8,128)(2,1)S(1)} %get-tuple-element.7.own), channel_id=1, source_target_pairs={{0,1},{1,0},{2,3},{3,2},{4,5},{5,4},{6,7},{7,6},{8,9},{9,8},{10,11... | collective-permute-start | bytes 897032 | tf_op jit(solution)/shard_map/ppermute | solution.py:311
  18.7 14.6 %collective-permute-start.4 = (bf16[1168,128]{1,0:T(8,128)(2,1)S(1)}, bf16[1168,128]{1,0:T(8,128)(2,1)S(1)}, u32[]{:S(2)}, u32[]{:S(2)}) collective-permute-start(bf16[1168,128]{1,0:T(8,128)(2,1)S(1)} %collective-permute-done.2.near_b), channel_id=1, source_target_pairs={{0,1},{1,0},{2,3},{3,2},{4,5},{5,4},{6,7},{7,6},{8,9},{9,8},{10,11... | collective-permute-start | bytes 897032 | tf_op jit(solution)/shard_map/ppermute | solution.py:311
  20.2 13.1 %collective-permute-start.3 = (bf16[1168,128]{1,0:T(8,128)(2,1)S(1)}, bf16[1168,128]{1,0:T(8,128)(2,1)S(1)}, u32[]{:S(2)}, u32[]{:S(2)}) collective-permute-start(bf16[1168,128]{1,0:T(8,128)(2,1)S(1)} %collective-permute-done.1.near_a), channel_id=1, source_target_pairs={{0,1},{1,0},{2,3},{3,2},{4,5},{5,4},{6,7},{7,6},{8,9},{9,8},{10,11... | collective-permute-start | bytes 897032 | tf_op jit(solution)/shard_map/ppermute | solution.py:311
  20.2 13.1 %collective-permute-start.5 = (bf16[912,128]{1,0:T(8,128)(2,1)S(1)}, bf16[912,128]{1,0:T(8,128)(2,1)S(1)}, u32[]{:S(2)}, u32[]{:S(2)}) collective-permute-start(bf16[912,128]{1,0:T(8,128)(2,1)S(1)} %get-tuple-element.8), channel_id=1, source_target_pairs={{1,4},{3,6},{4,1},{5,8},{6,3},{7,10},{8,5},{9,12},{10,7},{11,14},{... | collective-permute-start | bytes 700424 | tf_op jit(solution)/shard_map/ppermute | solution.py:311

commit v3 on v2

--- a/solution.py
+++ b/solution.py
@@ -20,7 +20,6 @@
 ORDER = KMAX * BS
 PAY = 9 * BS + 16
 FAR = 7 * BS + 16
-LISTS = 9
 TILE = 256
 
 
@@ -46,11 +45,20 @@
     return jnp.where(r == c, 1.0, 0.0).astype(F32)
 
 
-def pack_kernel(meta, ham, ortho, pay, far, hs, os, sems):
-    first, core = meta[0], meta[1]
+def position():
+    device = lax.axis_index(AXES).astype(jnp.int32)
+    return device * OWN, device & 1, (device >> 1) & 1
+
+
+def pack_kernel(pattern, lists, ham, ortho, pay, far, keep, slot_of, hs, os, sems):
+    first, core, _ = position()
     copies = [
         pltpu.make_async_copy(ham.at[c, pl.ds(2, 3)], hs.at[c], sems.at[c]) for c in range(OWN)
-    ] + [pltpu.make_async_copy(ortho, os, sems.at[OWN])]
+    ] + [
+        pltpu.make_async_copy(ortho, os, sems.at[OWN]),
+        pltpu.make_async_copy(pattern, keep, sems.at[OWN + 1]),
+        pltpu.make_async_copy(lists, slot_of, sems.at[OWN + 2]),
+    ]
     for copy in copies:
         copy.start()
     for copy in copies:
@@ -59,7 +67,7 @@
     r = lax.broadcasted_iota(jnp.int32, (BS, BS), 0)
     c = lax.broadcasted_iota(jnp.int32, (BS, BS), 1)
     masked = [
-        [hs[j, k].astype(F32) * meta[3 + 3 * j + k].astype(F32) for k in range(3)]
+        [hs[j, k].astype(F32) * keep[j, k + 2].astype(F32) for k in range(3)]
         for j in range(OWN)
     ]
     pay[rows(0), :] = jnp.where(r >= c, masked[0][0], masked[1][0]).astype(BF)
@@ -75,8 +83,8 @@
     row = lax.broadcasted_iota(jnp.int32, (16, BS), 0)
     extra = jnp.where(row == 1, diagonal, 0.0)
     for s in range(KMAX):
-        slot = meta[LISTS + s]
-        value = jnp.where(slot >= 0, slot + 2, 0).astype(F32)
+        slot = slot_of[0, s]
+        value = jnp.where(slot >= 0, slot - first + BACK + 2, 0).astype(F32)
         extra = extra + jnp.where((lane == s) & (row == 0), value, 0.0)
     pay[PAY - 16 : PAY, :] = extra.astype(BF)
 
@@ -89,12 +97,14 @@
 
 
 def main_kernel(
-    meta, own, pair, near_a, near_b, cross_a, cross_b, far, out,
-    hl, zc, zl, gt, up, xs, ms, ys, pb, rt, ob, slots, sems,
+    lists, own, pair, near_a, near_b, cross_a, cross_b, far, out,
+    hb, zc, zl, gt, up, xs, ms, ys, pb, rt, ob, slots, slot_of, sems,
 ):
-    core, odd_chip = meta[1], meta[2]
-    r = lax.broadcasted_iota(jnp.int32, (BS, BS), 0)
-    c = lax.broadcasted_iota(jnp.int32, (BS, BS), 1)
+    first, core, odd_chip = position()
+    lists_copy = pltpu.make_async_copy(lists, slot_of, sems.at[0])
+    lists_copy.start()
+    row_at = lax.broadcasted_iota(jnp.int32, (BS, BS), 0)
+    lane_at = lax.broadcasted_iota(jnp.int32, (BS, BS), 1)
     ident = eye(BS, BS)
 
     def put_z(i, upper, diagonal):
@@ -104,18 +114,29 @@
         zl[i, :, BS:] = upper
         zl[i + 1, :, :BS] = diag
 
+    def put_h(i, k, block):
+        hb[i, rows(k + 1), BS:] = block
+        if i + 1 < SPAN:
+            hb[i + 1, rows(k), :BS] = block
+        if k == 1 and i + 1 < SPAN:
+            hb[i + 1, rows(0), BS:] = block.T
+
     def take(k, pay, from_far=None):
         i = 2 * k + BACK
         size = PAY if from_far is None else FAR
         both = pay[rows(0), :].astype(F32)
         turned = pay[rows(0), :].T.astype(F32)
         last = pay[size - 16 : size, :].astype(F32)[1:2, :]
-        hl[i, rows(0), :] = jnp.where(r >= c, both, turned).astype(BF)
-        hl[i + 1, rows(0), :] = jnp.where(
-            r < c, both, jnp.where(r > c, turned, jnp.broadcast_to(last, (BS, BS)))
-        ).astype(BF)
-        hl[i, rows(1, 2), :] = pay[rows(1, 2), :]
-        hl[i + 1, rows(1, 2), :] = pay[rows(3, 2), :]
+        put_h(i, 0, jnp.where(row_at >= lane_at, both, turned).astype(BF))
+        diagonal = jnp.where(
+            row_at < lane_at,
+            both,
+            jnp.where(row_at > lane_at, turned, jnp.broadcast_to(last, (BS, BS))),
+        )
+        put_h(i + 1, 0, diagonal.astype(BF))
+        for j in range(OWN):
+            for k in range(1, 3):
+                put_h(i + j, k, pay[rows(2 * j + k), :])
         put_z(i + 1, pay[rows(5), :], pay[rows(6), :])
         if from_far is None:
             put_z(i, pay[rows(7), :], pay[rows(8), :])
@@ -131,8 +152,6 @@
             slots[2 * KMAX + s] = jnp.where(value > 0, value, -1)
 
     take(0, own)
-    for s in range(OWN * KMAX):
-        slots[s] = meta[LISTS + s]
 
     def sides(near_l, cross_l, near_r, cross_r):
         @pl.when(core == 0)
@@ -164,15 +183,8 @@
         sides(near_a, cross_a, near_b, cross_b)
 
     for b in range(1, SPAN):
-        zu_t = zc[b, :BS, :].T
-        zd_t = zc[b, BS:, :].T
-        left = nt(zu_t, hl[b - 1])
-        right = nt(zd_t, hl[b])
-        edge = nn(zd_t, hl[b - 1, rows(1), :])
-        gt[b, :, rows(0)] = (left[:, rows(0)] + edge).astype(BF)
-        gt[b, :, rows(1)] = (left[:, rows(1)] + right[:, rows(0)]).astype(BF)
-        gt[b, :, rows(2)] = (left[:, rows(2)] + right[:, rows(1)]).astype(BF)
-        gt[b, :, rows(3)] = right[:, rows(2)].astype(BF)
+        hb[b, rows(3), :BS] = jnp.zeros((BS, BS), BF)
+        gt[b] = nt(zc[b].T, hb[b]).astype(BF)
     for b in range(1, SPAN):
         for k in range(RO + 1):
             if b + k < SPAN:
@@ -182,18 +194,32 @@
                     block = nn(gt[b, :, rows(k)], zc[b + k, :BS, :])
                 up[4 * b + k] = (-block).astype(BF)
 
+    lists_copy.wait()
+    for j in range(OWN):
+        for s in range(KMAX):
+            slot = slot_of[j, s]
+            slots[j * KMAX + s] = jnp.where(slot >= 0, slot - first + BACK, -1)
     pb[...] = jnp.zeros_like(pb)
 
-    def solve(c, carry):
+    tiles = [slice(i * TILE, (i + 1) * TILE) for i in range(ORDER // TILE)]
+    big = eye(TILE, TILE)
+    top = eye(TILE, BS)
+
+    def places(c):
         where_to = [slots[c * KMAX + s] for s in range(KMAX)]
-        live = [w >= 0 for w in where_to]
+        return where_to, [w >= 0 for w in where_to]
+
+    def assemble(c, result):
+        where_to, live = places(c)
         count = functools.reduce(lambda a, b: a + b, [v.astype(jnp.int32) for v in live])
         squares = jnp.zeros((BS, BS), F32)
+        x = xs.at[c % 2]
         for s in range(KMAX):
             block = up[jnp.where(live[s], 4 * where_to[s], 0)].astype(F32)
             entry = jnp.where(live[s], CHEM * ident + block, 0.0)
             squares = squares + entry * entry
-            xs[rows(s), rows(s)] = entry.astype(BF)
+            x[rows(s), rows(s)] = entry.astype(BF)
+            yield
             for t in range(s):
                 ws, wt = where_to[s], where_to[t]
                 lo, hi = jnp.minimum(ws, wt), jnp.maximum(ws, wt)
@@ -202,24 +228,26 @@
                 turned = block.T
                 block = jnp.where(valid, block, jnp.zeros_like(block))
                 turned = jnp.where(valid, turned, jnp.zeros_like(turned))
-                xs[rows(s), rows(t)] = jnp.where(ws >= wt, turned, block)
-                xs[rows(t), rows(s)] = jnp.where(ws >= wt, block, turned)
+                x[rows(s), rows(t)] = jnp.where(ws >= wt, turned, block)
+                x[rows(t), rows(s)] = jnp.where(ws >= wt, block, turned)
                 wide = block.astype(F32)
                 squares = squares + 2.0 * (wide * wide)
+                yield
         total = jnp.sum(squares, axis=(0, 1), keepdims=True)
         width = (jnp.maximum(count, 1) * BS).astype(F32)
         inverse = 1.0 / (2.0 * jnp.sqrt(total / width + 1e-06))
-        half = 0.5 * inverse * inverse
-
-        tiles = [slice(i * TILE, (i + 1) * TILE) for i in range(ORDER // TILE)]
-        big = eye(TILE, TILE)
-        src, dst = xs, ys
+        result.extend([inverse, 0.5 * inverse * inverse])
+
+    def solve(c, inverse, half):
+        where_to, live = places(c)
+        src, dst = xs.at[c % 2], ys
         for step in range(STEPS - 1):
             for i, m in enumerate(tiles):
                 for n in tiles[: i + 1]:
                     square = nn(src[m, :], src[:, n])
                     base = 1.5 * big if m == n else 0.0
                     ms[m, n] = (base - (half if step == 0 else 0.5) * square).astype(BF)
+                    yield
             for i, m in enumerate(tiles):
                 for n in tiles[: i + 1]:
                     value = nn(src[m, n.start :], ms[n.start :, n])
@@ -231,13 +259,13 @@
                     dst[m, n] = value
                     if m != n:
                         dst[n, m] = value.T
+                    yield
             src, dst = dst, src
-        top = eye(TILE, BS)
         for m in tiles:
             square = nn(src[m, :], src[:, :BS])
             base = 1.5 * top if m.start == 0 else 0.0
             ms[m, :BS] = (base - 0.5 * square).astype(BF)
-        lanes = pl.ds(pl.multiple_of(c * BS, BS), BS)
+            yield
         for i, m in enumerate(tiles):
             part = nn(src[m, :], ms[:, :BS])
             if i == 0:
@@ -246,10 +274,20 @@
             for h in range(TILE // BS):
                 s = i * (TILE // BS) + h
                 row = jnp.where(live[s], where_to[s], SPAN)
-                pb[pl.ds(pl.multiple_of(row * BS, BS), BS), lanes] = part[rows(h), :]
-        return carry
-
-    lax.fori_loop(0, OWN + 1, solve, 0)
+                pb[pl.ds(pl.multiple_of(row * BS, BS), BS), rows(c)] = part[rows(h), :]
+            yield
+
+    scales = []
+    for _ in assemble(0, scales):
+        pass
+    for c in range(OWN + 1):
+        following = []
+        coming = assemble(c + 1, following) if c < OWN else iter(())
+        for _ in solve(c, *scales):
+            next(coming, None)
+        for _ in coming:
+            pass
+        scales = following
 
     for j in range(OWN):
         rt[:, rows(j)] = nt(pb[BS : SPAN * BS, rows(j, 2)], zl[BACK + j + 1]).astype(BF)
@@ -275,18 +313,19 @@
 
 def scratch():
     return [
-        pltpu.VMEM((SPAN, 3 * BS, BS), BF),
+        pltpu.VMEM((SPAN, 4 * BS, 2 * BS), BF),
         pltpu.VMEM((SPAN, 2 * BS, BS), BF),
         pltpu.VMEM((SPAN + 1, BS, 2 * BS), BF),
         pltpu.VMEM((SPAN, BS, 4 * BS), BF),
         pltpu.VMEM((4 * SPAN, BS, BS), BF),
-        pltpu.VMEM((ORDER, ORDER), BF),
+        pltpu.VMEM((2, ORDER, ORDER), BF),
         pltpu.VMEM((ORDER, ORDER), BF),
         pltpu.VMEM((ORDER, ORDER), BF),
         pltpu.VMEM(((SPAN + 1) * BS, 3 * BS), BF),
         pltpu.VMEM(((SPAN - 1) * BS, 2 * BS), BF),
         pltpu.VMEM((OWN, 13, BS, BS), F32),
         pltpu.SMEM((3 * KMAX,), jnp.int32),
+        pltpu.SMEM((OWN, KMAX), jnp.int32),
         pltpu.SemaphoreType.DMA((OWN * 13,)),
     ]
 
@@ -312,32 +351,24 @@
 
     in_hbm = lambda x: x if interpret else pltpu.with_memory_space_constraint(x, pltpu.HBM)
     vmem = pl.BlockSpec(memory_space=pltpu.VMEM)
-    smem = pl.BlockSpec(memory_space=pltpu.SMEM)
     anywhere = pl.BlockSpec(memory_space=pltpu.HBM)
 
     def local(hamiltonian, pattern, ortho, lists):
-        device = lax.axis_index(AXES).astype(jnp.int32)
-        first = device * OWN
-        meta = jnp.concatenate(
-            [
-                jnp.stack([first, device & 1, (device >> 1) & 1]),
-                pattern[:, 2:].reshape(-1),
-                jnp.where(lists >= 0, lists - first + BACK, -1).reshape(-1),
-            ]
-        )
         pay, far = pl.pallas_call(
             pack_kernel,
             out_shape=(jax.ShapeDtypeStruct((PAY, BS), BF), jax.ShapeDtypeStruct((FAR, BS), BF)),
-            in_specs=[smem, anywhere, anywhere],
+            in_specs=[anywhere] * 4,
             out_specs=(vmem, vmem),
             scratch_shapes=[
+                pltpu.SMEM(pattern.shape, jnp.int32),
+                pltpu.SMEM(lists.shape, jnp.int32),
                 pltpu.VMEM((OWN, 3, BS, BS), BF),
                 pltpu.VMEM((OWN, 2, BS, BS), BF),
-                pltpu.SemaphoreType.DMA((OWN + 1,)),
+                pltpu.SemaphoreType.DMA((OWN + 3,)),
             ],
             compiler_params=pltpu.CompilerParams(vmem_limit_bytes=8 << 20),
             interpret=interpret,
-        )(meta, in_hbm(hamiltonian), in_hbm(ortho))
+        )(in_hbm(pattern), in_hbm(lists), in_hbm(hamiltonian), in_hbm(ortho))
         near_b = send(pay, chips(1))
         near_a = send(pay, chips(0))
         got_far = send(far, cross)
@@ -347,7 +378,7 @@
         out = pl.pallas_call(
             main_kernel,
             out_shape=jax.ShapeDtypeStruct((OWN, 13, BS, BS), F32),
-            in_specs=[smem] + [vmem] * 7,
+            in_specs=[anywhere] + [vmem] * 7,
             out_specs=anywhere,
             scratch_shapes=scratch(),
             compiler_params=pltpu.CompilerParams(vmem_limit_bytes=24 << 20),
@@ -355,7 +386,7 @@
                 flops=12 * 10**9, bytes_accessed=4 << 20, transcendentals=0
             ),
             interpret=interpret,
-        )(meta, pay, pair, near_a, near_b, cross_a, cross_b, got_far)
+        )(in_hbm(lists), pay, pair, near_a, near_b, cross_a, cross_b, got_far)
         return out
 
     spec4 = P(AXES, None, None, None)

time: 49.7 us -> 47 us (0.946)
  Pallas kernels: 17.8 us -> 16.7 us
  local copies, waits for them, and re-layouts: 0.99 us -> 0 us
  other arithmetic: 0.68 us -> 0 us
    slice x1 -> x0, local copies, waits for them, and re-layouts: 0.75 us -> none  [local(): pattern[:, 2:].reshape(-1)]
    select_n x1 -> x0, other arithmetic: 0.68 us -> none  [local(): jnp.where(lists >= 0, lists - first + BACK, -1).reshape(-1)]
    pallas_call x1, Pallas kernels: 16.1 us -> 15.5 us  [local(): pl.pallas_call(main_kernel, out_shape=jax.ShapeDtypeStruct((OWN, 13, BS,...]
    pallas_call x1, Pallas kernels: 1.67 us -> 1.15 us  [local(): pl.pallas_call(pack_kernel, out_shape=(jax.ShapeDtypeStruct((PAY, BS), BF...]
where the time goes in v3:
time: 47 us; the launch traced here: 46.8 us
  waiting for transfers between devices  19.8 us (42%)
  Pallas kernels  16.7 us (36%)
  starting transfers between devices  10.1 us (21%)
    ppermute x6, waiting for transfers between devices, send(): return lax.ppermute(value, AXES, pairs)  19.8 us
    pallas_call x1, Pallas kernels, local(): pl.pallas_call(main_kernel, out_shape=jax.ShapeDtypeStruct((OWN, 13, BS,...  15.5 us
    ppermute x6, starting transfers between devices, send(): return lax.ppermute(value, AXES, pairs)  10.1 us
    pallas_call x1, Pallas kernels, local(): pl.pallas_call(pack_kernel, out_shape=(jax.ShapeDtypeStruct((PAY, BS), BF...  1.15 us
  transfers between devices with their start and end apart: 6, of which 2 were waited for; matrix products, arithmetic and copies ran while one was open for 0% of the time, Pallas kernels for 0%

profile of v3, /device:TPU:127, one launch (start us, length us, event | category | flops | bytes accessed | tf_op | source)
XLA Modules:
  0.0 46.8 jit_solution(2996337222383078331)
XLA Ops:
  0.0 1.1 %shard_map.46 = (bf16[1168,128]{1,0:T(8,128)(2,1)S(1)}, bf16[912,128]{1,0:T(8,128)(2,1)S(1)}) custom-call(s32[2,5]{1,0:T(2,128)} %pattern.1, s32[2,6]{1,0:T(2,128)} %lists.3, bf16[2,5,128,128]{3,2,1,0:T(8,128)(2,1)} %ham.1, bf16[2,2,128,128]{3,2,1,0:T(8,128)(2,1)} %ortho.1), custom_call_target="tpu_custom_call" | custom-call | tf_op jit(solution)/shard_map/pallas_call | solution.py:357
  1.2 4.3 %collective-permute-start.2 = (bf16[1168,128]{1,0:T(8,128)(2,1)S(1)}, bf16[1168,128]{1,0:T(8,128)(2,1)S(1)}, u32[]{:S(2)}, u32[]{:S(2)}) collective-permute-start(bf16[1168,128]{1,0:T(8,128)(2,1)S(1)} %get-tuple-element.7.own), channel_id=1, source_target_pairs={{2,4},{3,5},{4,2},{5,3},{6,8},{7,9},{8,6},{9,7},{10,12},{11,13},{1... | collective-permute-start | bytes 897032 | tf_op jit(solution)/shard_map/ppermute | solution.py:350
  5.5 0.1 collective-permute-start.1
  5.6 1.0 %collective-permute-start = (bf16[1168,128]{1,0:T(8,128)(2,1)S(1)}, bf16[1168,128]{1,0:T(8,128)(2,1)S(1)}, u32[]{:S(2)}, u32[]{:S(2)}) collective-permute-start(bf16[1168,128]{1,0:T(8,128)(2,1)S(1)} %get-tuple-element.7.own), channel_id=1, source_target_pairs={{0,1},{1,0},{2,3},{3,2},{4,5},{5,4},{6,7},{7,6},{8,9},{9,8},{10,11... | collective-permute-start | bytes 897032 | tf_op jit(solution)/shard_map/ppermute | solution.py:350
  6.6 9.8 %collective-permute-done.2.near_b = bf16[1168,128]{1,0:T(8,128)(2,1)S(1)} collective-permute-done((bf16[1168,128]{1,0:T(8,128)(2,1)S(1)}, bf16[1168,128]{1,0:T(8,128)(2,1)S(1)}, u32[]{:S(2)}, u32[]{:S(2)}) %collective-permute-start.2) | collective-permute-done | bytes 299040 | tf_op jit(solution)/shard_map/ppermute | solution.py:350
  16.5 1.5 %collective-permute-start.4 = (bf16[1168,128]{1,0:T(8,128)(2,1)S(1)}, bf16[1168,128]{1,0:T(8,128)(2,1)S(1)}, u32[]{:S(2)}, u32[]{:S(2)}) collective-permute-start(bf16[1168,128]{1,0:T(8,128)(2,1)S(1)} %collective-permute-done.2.near_b), channel_id=1, source_target_pairs={{0,1},{1,0},{2,3},{3,2},{4,5},{5,4},{6,7},{7,6},{8,9},{9,8},{10,11... | collective-permute-start | bytes 897032 | tf_op jit(solution)/shard_map/ppermute | solution.py:350
  18.0 0.0 collective-permute-done.1.near_a
  18.0 0.0 collective-permute-start.3
  18.0 3.1 %collective-permute-start.5 = (bf16[912,128]{1,0:T(8,128)(2,1)S(1)}, bf16[912,128]{1,0:T(8,128)(2,1)S(1)}, u32[]{:S(2)}, u32[]{:S(2)}) collective-permute-start(bf16[912,128]{1,0:T(8,128)(2,1)S(1)} %get-tuple-element.8), channel_id=1, source_target_pairs={{1,4},{3,6},{4,1},{5,8},{6,3},{7,10},{8,5},{9,12},{10,7},{11,14},{... | collective-permute-start | bytes 700424 | tf_op jit(solution)/shard_map/ppermute | solution.py:350
  21.1 10.0 %collective-permute-done.5.far = bf16[912,128]{1,0:T(8,128)(2,1)S(1)} collective-permute-done((bf16[912,128]{1,0:T(8,128)(2,1)S(1)}, bf16[912,128]{1,0:T(8,128)(2,1)S(1)}, u32[]{:S(2)}, u32[]{:S(2)}) %collective-permute-start.5) | collective-permute-done | bytes 233504 | tf_op jit(solution)/shard_map/ppermute | solution.py:350
  31.1 0.0 collective-permute-done.pair
  31.1 0.0 collective-permute-done.4.cross_b
  31.1 0.0 collective-permute-done.3.cross_a
  31.1 15.5 %shard_map.47 = f32[2,13,128,128]{3,2,1,0:T(8,128)} custom-call(s32[2,6]{1,0:T(2,128)} %lists.3, bf16[1168,128]{1,0:T(8,128)(2,1)S(1)} %get-tuple-element.7.own, bf16[1168,128]{1,0:T(8,128)(2,1)S(1)} %collective-permute-done.pair, bf16[1168,128]{1,0:T(8,128)(2,1)S(1)} %collective-permute-done.1.near_a, bf16[1168,128]{1,0:T(8,128)(2,1)S(1)} %collective-permute-done.2.near_b, ...), custom_call_target="tpu_custom_call" | custom-call | flops 12000000000 | bytes 4194304 | tf_op jit(solution)/shard_map/pallas_call | solution.py:378
Async XLA Ops:
  1.2 15.3 %collective-permute-start.2 = (bf16[1168,128]{1,0:T(8,128)(2,1)S(1)}, bf16[1168,128]{1,0:T(8,128)(2,1)S(1)}, u32[]{:S(2)}, u32[]{:S(2)}) collective-permute-start(bf16[1168,128]{1,0:T(8,128)(2,1)S(1)} %get-tuple-element.7.own), channel_id=1, source_target_pairs={{2,4},{3,5},{4,2},{5,3},{6,8},{7,9},{8,6},{9,7},{10,12},{11,13},{1... | collective-permute-start | bytes 897032 | tf_op jit(solution)/shard_map/ppermute | solution.py:350
  5.5 12.5 %collective-permute-start.1 = (bf16[1168,128]{1,0:T(8,128)(2,1)S(1)}, bf16[1168,128]{1,0:T(8,128)(2,1)S(1)}, u32[]{:S(2)}, u32[]{:S(2)}) collective-permute-start(bf16[1168,128]{1,0:T(8,128)(2,1)S(1)} %get-tuple-element.7.own), channel_id=1, source_target_pairs={{0,2},{1,3},{2,0},{3,1},{4,6},{5,7},{6,4},{7,5},{8,10},{9,11},{10,... | collective-permute-start | bytes 897032 | tf_op jit(solution)/shard_map/ppermute | solution.py:350
  5.6 25.5 %collective-permute-start = (bf16[1168,128]{1,0:T(8,128)(2,1)S(1)}, bf16[1168,128]{1,0:T(8,128)(2,1)S(1)}, u32[]{:S(2)}, u32[]{:S(2)}) collective-permute-start(bf16[1168,128]{1,0:T(8,128)(2,1)S(1)} %get-tuple-element.7.own), channel_id=1, source_target_pairs={{0,1},{1,0},{2,3},{3,2},{4,5},{5,4},{6,7},{7,6},{8,9},{9,8},{10,11... | collective-permute-start | bytes 897032 | tf_op jit(solution)/shard_map/ppermute | solution.py:350
  16.5 14.6 %collective-permute-start.4 = (bf16[1168,128]{1,0:T(8,128)(2,1)S(1)}, bf16[1168,128]{1,0:T(8,128)(2,1)S(1)}, u32[]{:S(2)}, u32[]{:S(2)}) collective-permute-start(bf16[1168,128]{1,0:T(8,128)(2,1)S(1)} %collective-permute-done.2.near_b), channel_id=1, source_target_pairs={{0,1},{1,0},{2,3},{3,2},{4,5},{5,4},{6,7},{7,6},{8,9},{9,8},{10,11... | collective-permute-start | bytes 897032 | tf_op jit(solution)/shard_map/ppermute | solution.py:350
  18.0 13.1 %collective-permute-start.3 = (bf16[1168,128]{1,0:T(8,128)(2,1)S(1)}, bf16[1168,128]{1,0:T(8,128)(2,1)S(1)}, u32[]{:S(2)}, u32[]{:S(2)}) collective-permute-start(bf16[1168,128]{1,0:T(8,128)(2,1)S(1)} %collective-permute-done.1.near_a), channel_id=1, source_target_pairs={{0,1},{1,0},{2,3},{3,2},{4,5},{5,4},{6,7},{7,6},{8,9},{9,8},{10,11... | collective-permute-start | bytes 897032 | tf_op jit(solution)/shard_map/ppermute | solution.py:350
  18.0 13.1 %collective-permute-start.5 = (bf16[912,128]{1,0:T(8,128)(2,1)S(1)}, bf16[912,128]{1,0:T(8,128)(2,1)S(1)}, u32[]{:S(2)}, u32[]{:S(2)}) collective-permute-start(bf16[912,128]{1,0:T(8,128)(2,1)S(1)} %get-tuple-element.8), channel_id=1, source_target_pairs={{1,4},{3,6},{4,1},{5,8},{6,3},{7,10},{8,5},{9,12},{10,7},{11,14},{... | collective-permute-start | bytes 700424 | tf_op jit(solution)/shard_map/ppermute | solution.py:350

commit v4 on v3

--- a/solution.py
+++ b/solution.py
@@ -203,7 +203,7 @@
 
     tiles = [slice(i * TILE, (i + 1) * TILE) for i in range(ORDER // TILE)]
     big = eye(TILE, TILE)
-    top = eye(TILE, BS)
+    top = eye(BS, ORDER)
 
     def places(c):
         where_to = [slots[c * KMAX + s] for s in range(KMAX)]
@@ -261,20 +261,14 @@
                         dst[n, m] = value.T
                     yield
             src, dst = dst, src
-        for m in tiles:
-            square = nn(src[m, :], src[:, :BS])
-            base = 1.5 * top if m.start == 0 else 0.0
-            ms[m, :BS] = (base - 0.5 * square).astype(BF)
-            yield
-        for i, m in enumerate(tiles):
-            part = nn(src[m, :], ms[:, :BS])
-            if i == 0:
-                part = part + top
-            part = (0.5 * part).astype(BF)
-            for h in range(TILE // BS):
-                s = i * (TILE // BS) + h
-                row = jnp.where(live[s], where_to[s], SPAN)
-                pb[pl.ds(pl.multiple_of(row * BS, BS), BS), rows(c)] = part[rows(h), :]
+        square = nn(src[:BS, :], src[...])
+        ms[:BS, :] = (1.5 * top - 0.5 * square).astype(BF)
+        yield
+        part = nn(ms[:BS, :], src[...])
+        part = (0.5 * (top + part)).astype(BF)
+        for s in range(KMAX):
+            place = jnp.where(live[s], where_to[s], SPAN)
+            pb[rows(c), pl.ds(pl.multiple_of(place * BS, BS), BS)] = part[:, rows(s)]
             yield
 
     scales = []
@@ -290,15 +284,15 @@
         scales = following
 
     for j in range(OWN):
-        rt[:, rows(j)] = nt(pb[BS : SPAN * BS, rows(j, 2)], zl[BACK + j + 1]).astype(BF)
+        rt[rows(j), :] = nn(zl[BACK + j + 1], pb[rows(j, 2), BS : SPAN * BS]).astype(BF)
     copies = []
     for i in range(SPAN):
         if i == 0:
-            part = nn(zl[1, :, BS:], rt[rows(0), :])
+            part = nt(zl[1, :, BS:], rt[:, rows(0)])
         elif i == SPAN - 1:
-            part = nn(zl[i + 1, :, :BS], rt[rows(i - 1), :])
+            part = nt(zl[i + 1, :, :BS], rt[:, rows(i - 1)])
         else:
-            part = nn(zl[i + 1], rt[rows(i - 1, 2), :])
+            part = nt(zl[i + 1], rt[:, rows(i - 1, 2)])
         for j in range(OWN):
             if 0 <= i - j < 13:
                 ob[j, i - j] = part[:, rows(j)]
@@ -321,8 +315,8 @@
         pltpu.VMEM((2, ORDER, ORDER), BF),
         pltpu.VMEM((ORDER, ORDER), BF),
         pltpu.VMEM((ORDER, ORDER), BF),
-        pltpu.VMEM(((SPAN + 1) * BS, 3 * BS), BF),
-        pltpu.VMEM(((SPAN - 1) * BS, 2 * BS), BF),
+        pltpu.VMEM((3 * BS, (SPAN + 1) * BS), BF),
+        pltpu.VMEM((2 * BS, (SPAN - 1) * BS), BF),
         pltpu.VMEM((OWN, 13, BS, BS), F32),
         pltpu.SMEM((3 * KMAX,), jnp.int32),
         pltpu.SMEM((OWN, KMAX), jnp.int32),

time: 47 us -> 45.7 us (0.972)
  Pallas kernels: 16.7 us -> 15.4 us
    pallas_call x1, Pallas kernels: 15.5 us -> 14.2 us  [local(): pl.pallas_call(main_kernel, out_shape=jax.ShapeDtypeStruct((OWN, 13, BS,...]
where the time goes in v4:
time: 45.7 us; the launch traced here: 45.5 us
  waiting for transfers between devices  19.8 us (43%)
  Pallas kernels  15.4 us (34%)
  starting transfers between devices  10.1 us (22%)
    ppermute x6, waiting for transfers between devices, send(): return lax.ppermute(value, AXES, pairs)  19.8 us
    pallas_call x1, Pallas kernels, local(): pl.pallas_call(main_kernel, out_shape=jax.ShapeDtypeStruct((OWN, 13, BS,...  14.2 us
    ppermute x6, starting transfers between devices, send(): return lax.ppermute(value, AXES, pairs)  10.1 us
    pallas_call x1, Pallas kernels, local(): pl.pallas_call(pack_kernel, out_shape=(jax.ShapeDtypeStruct((PAY, BS), BF...  1.15 us
  transfers between devices with their start and end apart: 6, of which 2 were waited for; matrix products, arithmetic and copies ran while one was open for 0% of the time, Pallas kernels for 0%

profile of v4, /device:TPU:127, one launch (start us, length us, event | category | flops | bytes accessed | tf_op | source)
XLA Modules:
  0.0 45.5 jit_solution(10944093511934122675)
XLA Ops:
  0.0 1.1 %shard_map.46 = (bf16[1168,128]{1,0:T(8,128)(2,1)S(1)}, bf16[912,128]{1,0:T(8,128)(2,1)S(1)}) custom-call(s32[2,5]{1,0:T(2,128)} %pattern.1, s32[2,6]{1,0:T(2,128)} %lists.3, bf16[2,5,128,128]{3,2,1,0:T(8,128)(2,1)} %ham.1, bf16[2,2,128,128]{3,2,1,0:T(8,128)(2,1)} %ortho.1), custom_call_target="tpu_custom_call" | custom-call | tf_op jit(solution)/shard_map/pallas_call | solution.py:351
  1.2 4.3 %collective-permute-start.2 = (bf16[1168,128]{1,0:T(8,128)(2,1)S(1)}, bf16[1168,128]{1,0:T(8,128)(2,1)S(1)}, u32[]{:S(2)}, u32[]{:S(2)}) collective-permute-start(bf16[1168,128]{1,0:T(8,128)(2,1)S(1)} %get-tuple-element.7.own), channel_id=1, source_target_pairs={{2,4},{3,5},{4,2},{5,3},{6,8},{7,9},{8,6},{9,7},{10,12},{11,13},{1... | collective-permute-start | bytes 897032 | tf_op jit(solution)/shard_map/ppermute | solution.py:344
  5.5 0.1 collective-permute-start.1
  5.6 1.0 %collective-permute-start = (bf16[1168,128]{1,0:T(8,128)(2,1)S(1)}, bf16[1168,128]{1,0:T(8,128)(2,1)S(1)}, u32[]{:S(2)}, u32[]{:S(2)}) collective-permute-start(bf16[1168,128]{1,0:T(8,128)(2,1)S(1)} %get-tuple-element.7.own), channel_id=1, source_target_pairs={{0,1},{1,0},{2,3},{3,2},{4,5},{5,4},{6,7},{7,6},{8,9},{9,8},{10,11... | collective-permute-start | bytes 897032 | tf_op jit(solution)/shard_map/ppermute | solution.py:344
  6.6 9.8 %collective-permute-done.2.near_b = bf16[1168,128]{1,0:T(8,128)(2,1)S(1)} collective-permute-done((bf16[1168,128]{1,0:T(8,128)(2,1)S(1)}, bf16[1168,128]{1,0:T(8,128)(2,1)S(1)}, u32[]{:S(2)}, u32[]{:S(2)}) %collective-permute-start.2) | collective-permute-done | bytes 299040 | tf_op jit(solution)/shard_map/ppermute | solution.py:344
  16.5 1.5 %collective-permute-start.4 = (bf16[1168,128]{1,0:T(8,128)(2,1)S(1)}, bf16[1168,128]{1,0:T(8,128)(2,1)S(1)}, u32[]{:S(2)}, u32[]{:S(2)}) collective-permute-start(bf16[1168,128]{1,0:T(8,128)(2,1)S(1)} %collective-permute-done.2.near_b), channel_id=1, source_target_pairs={{0,1},{1,0},{2,3},{3,2},{4,5},{5,4},{6,7},{7,6},{8,9},{9,8},{10,11... | collective-permute-start | bytes 897032 | tf_op jit(solution)/shard_map/ppermute | solution.py:344
  18.0 0.0 collective-permute-done.1.near_a
  18.0 0.0 collective-permute-start.3
  18.0 3.1 %collective-permute-start.5 = (bf16[912,128]{1,0:T(8,128)(2,1)S(1)}, bf16[912,128]{1,0:T(8,128)(2,1)S(1)}, u32[]{:S(2)}, u32[]{:S(2)}) collective-permute-start(bf16[912,128]{1,0:T(8,128)(2,1)S(1)} %get-tuple-element.8), channel_id=1, source_target_pairs={{1,4},{3,6},{4,1},{5,8},{6,3},{7,10},{8,5},{9,12},{10,7},{11,14},{... | collective-permute-start | bytes 700424 | tf_op jit(solution)/shard_map/ppermute | solution.py:344
  21.1 10.0 %collective-permute-done.5.far = bf16[912,128]{1,0:T(8,128)(2,1)S(1)} collective-permute-done((bf16[912,128]{1,0:T(8,128)(2,1)S(1)}, bf16[912,128]{1,0:T(8,128)(2,1)S(1)}, u32[]{:S(2)}, u32[]{:S(2)}) %collective-permute-start.5) | collective-permute-done | bytes 233504 | tf_op jit(solution)/shard_map/ppermute | solution.py:344
  31.1 0.0 collective-permute-done.pair
  31.1 0.0 collective-permute-done.4.cross_b
  31.1 0.0 collective-permute-done.3.cross_a
  31.1 14.2 %shard_map.47 = f32[2,13,128,128]{3,2,1,0:T(8,128)} custom-call(s32[2,6]{1,0:T(2,128)} %lists.3, bf16[1168,128]{1,0:T(8,128)(2,1)S(1)} %get-tuple-element.7.own, bf16[1168,128]{1,0:T(8,128)(2,1)S(1)} %collective-permute-done.pair, bf16[1168,128]{1,0:T(8,128)(2,1)S(1)} %collective-permute-done.1.near_a, bf16[1168,128]{1,0:T(8,128)(2,1)S(1)} %collective-permute-done.2.near_b, ...), custom_call_target="tpu_custom_call" | custom-call | flops 12000000000 | bytes 4194304 | tf_op jit(solution)/shard_map/pallas_call | solution.py:372
Async XLA Ops:
  1.2 15.3 %collective-permute-start.2 = (bf16[1168,128]{1,0:T(8,128)(2,1)S(1)}, bf16[1168,128]{1,0:T(8,128)(2,1)S(1)}, u32[]{:S(2)}, u32[]{:S(2)}) collective-permute-start(bf16[1168,128]{1,0:T(8,128)(2,1)S(1)} %get-tuple-element.7.own), channel_id=1, source_target_pairs={{2,4},{3,5},{4,2},{5,3},{6,8},{7,9},{8,6},{9,7},{10,12},{11,13},{1... | collective-permute-start | bytes 897032 | tf_op jit(solution)/shard_map/ppermute | solution.py:344
  5.5 12.5 %collective-permute-start.1 = (bf16[1168,128]{1,0:T(8,128)(2,1)S(1)}, bf16[1168,128]{1,0:T(8,128)(2,1)S(1)}, u32[]{:S(2)}, u32[]{:S(2)}) collective-permute-start(bf16[1168,128]{1,0:T(8,128)(2,1)S(1)} %get-tuple-element.7.own), channel_id=1, source_target_pairs={{0,2},{1,3},{2,0},{3,1},{4,6},{5,7},{6,4},{7,5},{8,10},{9,11},{10,... | collective-permute-start | bytes 897032 | tf_op jit(solution)/shard_map/ppermute | solution.py:344
  5.6 25.5 %collective-permute-start = (bf16[1168,128]{1,0:T(8,128)(2,1)S(1)}, bf16[1168,128]{1,0:T(8,128)(2,1)S(1)}, u32[]{:S(2)}, u32[]{:S(2)}) collective-permute-start(bf16[1168,128]{1,0:T(8,128)(2,1)S(1)} %get-tuple-element.7.own), channel_id=1, source_target_pairs={{0,1},{1,0},{2,3},{3,2},{4,5},{5,4},{6,7},{7,6},{8,9},{9,8},{10,11... | collective-permute-start | bytes 897032 | tf_op jit(solution)/shard_map/ppermute | solution.py:344
  16.5 14.6 %collective-permute-start.4 = (bf16[1168,128]{1,0:T(8,128)(2,1)S(1)}, bf16[1168,128]{1,0:T(8,128)(2,1)S(1)}, u32[]{:S(2)}, u32[]{:S(2)}) collective-permute-start(bf16[1168,128]{1,0:T(8,128)(2,1)S(1)} %collective-permute-done.2.near_b), channel_id=1, source_target_pairs={{0,1},{1,0},{2,3},{3,2},{4,5},{5,4},{6,7},{7,6},{8,9},{9,8},{10,11... | collective-permute-start | bytes 897032 | tf_op jit(solution)/shard_map/ppermute | solution.py:344
  18.0 13.1 %collective-permute-start.3 = (bf16[1168,128]{1,0:T(8,128)(2,1)S(1)}, bf16[1168,128]{1,0:T(8,128)(2,1)S(1)}, u32[]{:S(2)}, u32[]{:S(2)}) collective-permute-start(bf16[1168,128]{1,0:T(8,128)(2,1)S(1)} %collective-permute-done.1.near_a), channel_id=1, source_target_pairs={{0,1},{1,0},{2,3},{3,2},{4,5},{5,4},{6,7},{7,6},{8,9},{9,8},{10,11... | collective-permute-start | bytes 897032 | tf_op jit(solution)/shard_map/ppermute | solution.py:344
  18.0 13.1 %collective-permute-start.5 = (bf16[912,128]{1,0:T(8,128)(2,1)S(1)}, bf16[912,128]{1,0:T(8,128)(2,1)S(1)}, u32[]{:S(2)}, u32[]{:S(2)}) collective-permute-start(bf16[912,128]{1,0:T(8,128)(2,1)S(1)} %get-tuple-element.8), channel_id=1, source_target_pairs={{1,4},{3,6},{4,1},{5,8},{6,3},{7,10},{8,5},{9,12},{10,7},{11,14},{... | collective-permute-start | bytes 700424 | tf_op jit(solution)/shard_map/ppermute | solution.py:344

commit v5 on v4

--- a/solution.py
+++ b/solution.py
@@ -241,30 +241,45 @@
     def solve(c, inverse, half):
         where_to, live = places(c)
         src, dst = xs.at[c % 2], ys
+        pairs = [(m, n) for i, m in enumerate(tiles) for n in tiles[: i + 1]]
         for step in range(STEPS - 1):
-            for i, m in enumerate(tiles):
-                for n in tiles[: i + 1]:
-                    square = nn(src[m, :], src[:, n])
+            if step:
+                src, dst = dst, src
+            last = step == STEPS - 2
+            for m, n in pairs:
+                square = nn(src[m, :], src[:, n])
+                if last:
+                    value = square.astype(BF)
+                    ms[m, n] = value
+                    if m != n:
+                        ms[n, m] = value.T
+                else:
                     base = 1.5 * big if m == n else 0.0
                     ms[m, n] = (base - (half if step == 0 else 0.5) * square).astype(BF)
-                    yield
-            for i, m in enumerate(tiles):
-                for n in tiles[: i + 1]:
-                    value = nn(src[m, n.start :], ms[n.start :, n])
-                    if n.start:
-                        value = value + nt(src[m, : n.start], ms[n, : n.start])
-                    if step == 0:
-                        value = value * inverse
-                    value = value.astype(BF)
-                    dst[m, n] = value
-                    if m != n:
-                        dst[n, m] = value.T
-                    yield
-            src, dst = dst, src
-        square = nn(src[:BS, :], src[...])
-        ms[:BS, :] = (1.5 * top - 0.5 * square).astype(BF)
+                yield
+            if last:
+                break
+            for m, n in pairs:
+                value = nn(src[m, n.start :], ms[n.start :, n])
+                if n.start:
+                    value = value + nt(src[m, : n.start], ms[n, : n.start])
+                if step == 0:
+                    value = value * inverse
+                value = value.astype(BF)
+                dst[m, n] = value
+                if m != n:
+                    dst[n, m] = value.T
+                yield
+
+        def times_m(v):
+            return 1.5 * v - 0.5 * nn(v.astype(BF), ms[...])
+
+        first_m = 1.5 * top - 0.5 * ms[:BS, :].astype(F32)
+        square = nn(times_m(first_m).astype(BF), ms[...])
         yield
-        part = nn(ms[:BS, :], src[...])
+        after = times_m(1.5 * top - 0.5 * square)
+        yield
+        part = nn(after.astype(BF), src[...])
         part = (0.5 * (top + part)).astype(BF)
         for s in range(KMAX):
             place = jnp.where(live[s], where_to[s], SPAN)

time: 45.7 us -> 45.4 us (level)
  no operation moved by 1% of the time
where the time goes in v5:
time: 45.4 us; the launch traced here: 45.1 us
  waiting for transfers between devices  19.8 us (44%)
  Pallas kernels  15 us (33%)
  starting transfers between devices  10.1 us (22%)
    ppermute x6, waiting for transfers between devices, send(): return lax.ppermute(value, AXES, pairs)  19.8 us
    pallas_call x1, Pallas kernels, local(): pl.pallas_call(main_kernel, out_shape=jax.ShapeDtypeStruct((OWN, 13, BS,...  13.8 us
    ppermute x6, starting transfers between devices, send(): return lax.ppermute(value, AXES, pairs)  10.1 us
    pallas_call x1, Pallas kernels, local(): pl.pallas_call(pack_kernel, out_shape=(jax.ShapeDtypeStruct((PAY, BS), BF...  1.15 us
  transfers between devices with their start and end apart: 6, of which 2 were waited for; matrix products, arithmetic and copies ran while one was open for 0% of the time, Pallas kernels for 0%

profile of v5, /device:TPU:127, one launch (start us, length us, event | category | flops | bytes accessed | tf_op | source)
XLA Modules:
  0.0 45.1 jit_solution(1034693109796516303)
XLA Ops:
  0.0 1.1 %shard_map.46 = (bf16[1168,128]{1,0:T(8,128)(2,1)S(1)}, bf16[912,128]{1,0:T(8,128)(2,1)S(1)}) custom-call(s32[2,5]{1,0:T(2,128)} %pattern.1, s32[2,6]{1,0:T(2,128)} %lists.3, bf16[2,5,128,128]{3,2,1,0:T(8,128)(2,1)} %ham.1, bf16[2,2,128,128]{3,2,1,0:T(8,128)(2,1)} %ortho.1), custom_call_target="tpu_custom_call" | custom-call | tf_op jit(solution)/shard_map/pallas_call | solution.py:366
  1.2 4.3 %collective-permute-start.2 = (bf16[1168,128]{1,0:T(8,128)(2,1)S(1)}, bf16[1168,128]{1,0:T(8,128)(2,1)S(1)}, u32[]{:S(2)}, u32[]{:S(2)}) collective-permute-start(bf16[1168,128]{1,0:T(8,128)(2,1)S(1)} %get-tuple-element.7.own), channel_id=1, source_target_pairs={{2,4},{3,5},{4,2},{5,3},{6,8},{7,9},{8,6},{9,7},{10,12},{11,13},{1... | collective-permute-start | bytes 897032 | tf_op jit(solution)/shard_map/ppermute | solution.py:359
  5.5 0.1 collective-permute-start.1
  5.6 1.0 %collective-permute-start = (bf16[1168,128]{1,0:T(8,128)(2,1)S(1)}, bf16[1168,128]{1,0:T(8,128)(2,1)S(1)}, u32[]{:S(2)}, u32[]{:S(2)}) collective-permute-start(bf16[1168,128]{1,0:T(8,128)(2,1)S(1)} %get-tuple-element.7.own), channel_id=1, source_target_pairs={{0,1},{1,0},{2,3},{3,2},{4,5},{5,4},{6,7},{7,6},{8,9},{9,8},{10,11... | collective-permute-start | bytes 897032 | tf_op jit(solution)/shard_map/ppermute | solution.py:359
  6.6 9.8 %collective-permute-done.2.near_b = bf16[1168,128]{1,0:T(8,128)(2,1)S(1)} collective-permute-done((bf16[1168,128]{1,0:T(8,128)(2,1)S(1)}, bf16[1168,128]{1,0:T(8,128)(2,1)S(1)}, u32[]{:S(2)}, u32[]{:S(2)}) %collective-permute-start.2) | collective-permute-done | bytes 299040 | tf_op jit(solution)/shard_map/ppermute | solution.py:359
  16.5 1.5 %collective-permute-start.4 = (bf16[1168,128]{1,0:T(8,128)(2,1)S(1)}, bf16[1168,128]{1,0:T(8,128)(2,1)S(1)}, u32[]{:S(2)}, u32[]{:S(2)}) collective-permute-start(bf16[1168,128]{1,0:T(8,128)(2,1)S(1)} %collective-permute-done.2.near_b), channel_id=1, source_target_pairs={{0,1},{1,0},{2,3},{3,2},{4,5},{5,4},{6,7},{7,6},{8,9},{9,8},{10,11... | collective-permute-start | bytes 897032 | tf_op jit(solution)/shard_map/ppermute | solution.py:359
  18.0 0.0 collective-permute-done.1.near_a
  18.0 0.0 collective-permute-start.3
  18.0 3.1 %collective-permute-start.5 = (bf16[912,128]{1,0:T(8,128)(2,1)S(1)}, bf16[912,128]{1,0:T(8,128)(2,1)S(1)}, u32[]{:S(2)}, u32[]{:S(2)}) collective-permute-start(bf16[912,128]{1,0:T(8,128)(2,1)S(1)} %get-tuple-element.8), channel_id=1, source_target_pairs={{1,4},{3,6},{4,1},{5,8},{6,3},{7,10},{8,5},{9,12},{10,7},{11,14},{... | collective-permute-start | bytes 700424 | tf_op jit(solution)/shard_map/ppermute | solution.py:359
  21.1 10.0 %collective-permute-done.5.far = bf16[912,128]{1,0:T(8,128)(2,1)S(1)} collective-permute-done((bf16[912,128]{1,0:T(8,128)(2,1)S(1)}, bf16[912,128]{1,0:T(8,128)(2,1)S(1)}, u32[]{:S(2)}, u32[]{:S(2)}) %collective-permute-start.5) | collective-permute-done | bytes 233504 | tf_op jit(solution)/shard_map/ppermute | solution.py:359
  31.1 0.0 collective-permute-done.pair
  31.1 0.0 collective-permute-done.4.cross_b
  31.1 0.0 collective-permute-done.3.cross_a
  31.1 13.8 %shard_map.47 = f32[2,13,128,128]{3,2,1,0:T(8,128)} custom-call(s32[2,6]{1,0:T(2,128)} %lists.3, bf16[1168,128]{1,0:T(8,128)(2,1)S(1)} %get-tuple-element.7.own, bf16[1168,128]{1,0:T(8,128)(2,1)S(1)} %collective-permute-done.pair, bf16[1168,128]{1,0:T(8,128)(2,1)S(1)} %collective-permute-done.1.near_a, bf16[1168,128]{1,0:T(8,128)(2,1)S(1)} %collective-permute-done.2.near_b, ...), custom_call_target="tpu_custom_call" | custom-call | flops 12000000000 | bytes 4194304 | tf_op jit(solution)/shard_map/pallas_call | solution.py:387
Async XLA Ops:
  1.2 15.3 %collective-permute-start.2 = (bf16[1168,128]{1,0:T(8,128)(2,1)S(1)}, bf16[1168,128]{1,0:T(8,128)(2,1)S(1)}, u32[]{:S(2)}, u32[]{:S(2)}) collective-permute-start(bf16[1168,128]{1,0:T(8,128)(2,1)S(1)} %get-tuple-element.7.own), channel_id=1, source_target_pairs={{2,4},{3,5},{4,2},{5,3},{6,8},{7,9},{8,6},{9,7},{10,12},{11,13},{1... | collective-permute-start | bytes 897032 | tf_op jit(solution)/shard_map/ppermute | solution.py:359
  5.5 12.5 %collective-permute-start.1 = (bf16[1168,128]{1,0:T(8,128)(2,1)S(1)}, bf16[1168,128]{1,0:T(8,128)(2,1)S(1)}, u32[]{:S(2)}, u32[]{:S(2)}) collective-permute-start(bf16[1168,128]{1,0:T(8,128)(2,1)S(1)} %get-tuple-element.7.own), channel_id=1, source_target_pairs={{0,2},{1,3},{2,0},{3,1},{4,6},{5,7},{6,4},{7,5},{8,10},{9,11},{10,... | collective-permute-start | bytes 897032 | tf_op jit(solution)/shard_map/ppermute | solution.py:359
  5.6 25.5 %collective-permute-start = (bf16[1168,128]{1,0:T(8,128)(2,1)S(1)}, bf16[1168,128]{1,0:T(8,128)(2,1)S(1)}, u32[]{:S(2)}, u32[]{:S(2)}) collective-permute-start(bf16[1168,128]{1,0:T(8,128)(2,1)S(1)} %get-tuple-element.7.own), channel_id=1, source_target_pairs={{0,1},{1,0},{2,3},{3,2},{4,5},{5,4},{6,7},{7,6},{8,9},{9,8},{10,11... | collective-permute-start | bytes 897032 | tf_op jit(solution)/shard_map/ppermute | solution.py:359
  16.5 14.6 %collective-permute-start.4 = (bf16[1168,128]{1,0:T(8,128)(2,1)S(1)}, bf16[1168,128]{1,0:T(8,128)(2,1)S(1)}, u32[]{:S(2)}, u32[]{:S(2)}) collective-permute-start(bf16[1168,128]{1,0:T(8,128)(2,1)S(1)} %collective-permute-done.2.near_b), channel_id=1, source_target_pairs={{0,1},{1,0},{2,3},{3,2},{4,5},{5,4},{6,7},{7,6},{8,9},{9,8},{10,11... | collective-permute-start | bytes 897032 | tf_op jit(solution)/shard_map/ppermute | solution.py:359
  18.0 13.1 %collective-permute-start.3 = (bf16[1168,128]{1,0:T(8,128)(2,1)S(1)}, bf16[1168,128]{1,0:T(8,128)(2,1)S(1)}, u32[]{:S(2)}, u32[]{:S(2)}) collective-permute-start(bf16[1168,128]{1,0:T(8,128)(2,1)S(1)} %collective-permute-done.1.near_a), channel_id=1, source_target_pairs={{0,1},{1,0},{2,3},{3,2},{4,5},{5,4},{6,7},{7,6},{8,9},{9,8},{10,11... | collective-permute-start | bytes 897032 | tf_op jit(solution)/shard_map/ppermute | solution.py:359
  18.0 13.1 %collective-permute-start.5 = (bf16[912,128]{1,0:T(8,128)(2,1)S(1)}, bf16[912,128]{1,0:T(8,128)(2,1)S(1)}, u32[]{:S(2)}, u32[]{:S(2)}) collective-permute-start(bf16[912,128]{1,0:T(8,128)(2,1)S(1)} %get-tuple-element.8), channel_id=1, source_target_pairs={{1,4},{3,6},{4,1},{5,8},{6,3},{7,10},{8,5},{9,12},{10,7},{11,14},{... | collective-permute-start | bytes 700424 | tf_op jit(solution)/shard_map/ppermute | solution.py:359

commit v6 on v5

--- a/solution.py
+++ b/solution.py
@@ -50,16 +50,20 @@
     return device * OWN, device & 1, (device >> 1) & 1
 
 
-def pack_kernel(pattern, lists, ham, ortho, pay, far, keep, slot_of, hs, os, sems):
+def pack_kernel(pattern, lists, ham, ortho, pay, far, keep, slot_of, hs, sems):
     first, core, _ = position()
     copies = [
         pltpu.make_async_copy(ham.at[c, pl.ds(2, 3)], hs.at[c], sems.at[c]) for c in range(OWN)
     ] + [
-        pltpu.make_async_copy(ortho, os, sems.at[OWN]),
-        pltpu.make_async_copy(pattern, keep, sems.at[OWN + 1]),
-        pltpu.make_async_copy(lists, slot_of, sems.at[OWN + 2]),
+        pltpu.make_async_copy(pattern, keep, sems.at[OWN]),
+        pltpu.make_async_copy(lists, slot_of, sems.at[OWN + 1]),
     ]
-    for copy in copies:
+    places = [(pay, 5, 1, 0), (pay, 6, 1, 1), (pay, 7, 0, 0), (pay, 8, 0, 1), (far, 5, 1, 0), (far, 6, 1, 1)]
+    straight = [
+        pltpu.make_async_copy(ortho.at[j, k], to.at[pl.ds(i * BS, BS)], sems.at[OWN + 2 + n])
+        for n, (to, i, j, k) in enumerate(places)
+    ]
+    for copy in copies + straight:
         copy.start()
     for copy in copies:
         copy.wait()
@@ -74,10 +78,6 @@
     for j in range(OWN):
         for k in range(1, 3):
             pay[rows(2 * j + k), :] = masked[j][k].astype(BF)
-    pay[rows(5), :] = os[1, 0]
-    pay[rows(6), :] = os[1, 1]
-    pay[rows(7), :] = (os[0, 0].astype(F32) * jnp.where(first == 0, 0.0, 1.0)).astype(BF)
-    pay[rows(8), :] = os[0, 1]
     diagonal = jnp.sum(jnp.where(r == c, masked[1][0], 0.0), axis=0, keepdims=True)
     lane = lax.broadcasted_iota(jnp.int32, (16, BS), 1)
     row = lax.broadcasted_iota(jnp.int32, (16, BS), 0)
@@ -88,8 +88,14 @@
         extra = extra + jnp.where((lane == s) & (row == 0), value, 0.0)
     pay[PAY - 16 : PAY, :] = extra.astype(BF)
 
-    far[rows(0, 7), :] = pay[rows(0, 7), :]
+    far[rows(0, 5), :] = pay[rows(0, 5), :]
     far[FAR - 16 : FAR, :] = extra.astype(BF)
+    for copy in straight:
+        copy.wait()
+
+    @pl.when(first == 0)
+    def _():
+        pay[rows(7), :] = jnp.zeros((BS, BS), BF)
 
     @pl.when(core == 0)
     def _():
@@ -372,8 +378,7 @@
                 pltpu.SMEM(pattern.shape, jnp.int32),
                 pltpu.SMEM(lists.shape, jnp.int32),
                 pltpu.VMEM((OWN, 3, BS, BS), BF),
-                pltpu.VMEM((OWN, 2, BS, BS), BF),
-                pltpu.SemaphoreType.DMA((OWN + 3,)),
+                pltpu.SemaphoreType.DMA((OWN + 8,)),
             ],
             compiler_params=pltpu.CompilerParams(vmem_limit_bytes=8 << 20),
             interpret=interpret,

time: 45.4 us -> 45.3 us (level)
  no operation moved by 1% of the time
where the time goes in v6:
time: 45.3 us; the launch traced here: 45.1 us
  waiting for transfers between devices  19.8 us (44%)
  Pallas kernels  15 us (33%)
  starting transfers between devices  10.1 us (22%)
    ppermute x6, waiting for transfers between devices, send(): return lax.ppermute(value, AXES, pairs)  19.8 us
    pallas_call x1, Pallas kernels, local(): pl.pallas_call(main_kernel, out_shape=jax.ShapeDtypeStruct((OWN, 13, BS,...  13.8 us
    ppermute x6, starting transfers between devices, send(): return lax.ppermute(value, AXES, pairs)  10.1 us
    pallas_call x1, Pallas kernels, local(): pl.pallas_call(pack_kernel, out_shape=(jax.ShapeDtypeStruct((PAY, BS), BF...  1.13 us
  transfers between devices with their start and end apart: 6, of which 2 were waited for; matrix products, arithmetic and copies ran while one was open for 0% of the time, Pallas kernels for 0%

profile of v6, /device:TPU:127, one launch (start us, length us, event | category | flops | bytes accessed | tf_op | source)
XLA Modules:
  0.0 45.1 jit_solution(1110780981959352029)
XLA Ops:
  0.0 1.1 %shard_map.46 = (bf16[1168,128]{1,0:T(8,128)(2,1)S(1)}, bf16[912,128]{1,0:T(8,128)(2,1)S(1)}) custom-call(s32[2,5]{1,0:T(2,128)} %pattern.1, s32[2,6]{1,0:T(2,128)} %lists.3, bf16[2,5,128,128]{3,2,1,0:T(8,128)(2,1)} %ham.1, bf16[2,2,128,128]{3,2,1,0:T(8,128)(2,1)} %ortho.1), custom_call_target="tpu_custom_call" | custom-call | tf_op jit(solution)/shard_map/pallas_call | solution.py:372
  1.1 4.3 %collective-permute-start.2 = (bf16[1168,128]{1,0:T(8,128)(2,1)S(1)}, bf16[1168,128]{1,0:T(8,128)(2,1)S(1)}, u32[]{:S(2)}, u32[]{:S(2)}) collective-permute-start(bf16[1168,128]{1,0:T(8,128)(2,1)S(1)} %get-tuple-element.7.own), channel_id=1, source_target_pairs={{2,4},{3,5},{4,2},{5,3},{6,8},{7,9},{8,6},{9,7},{10,12},{11,13},{1... | collective-permute-start | bytes 897032 | tf_op jit(solution)/shard_map/ppermute | solution.py:365
  5.5 0.1 collective-permute-start.1
  5.6 1.0 %collective-permute-start = (bf16[1168,128]{1,0:T(8,128)(2,1)S(1)}, bf16[1168,128]{1,0:T(8,128)(2,1)S(1)}, u32[]{:S(2)}, u32[]{:S(2)}) collective-permute-start(bf16[1168,128]{1,0:T(8,128)(2,1)S(1)} %get-tuple-element.7.own), channel_id=1, source_target_pairs={{0,1},{1,0},{2,3},{3,2},{4,5},{5,4},{6,7},{7,6},{8,9},{9,8},{10,11... | collective-permute-start | bytes 897032 | tf_op jit(solution)/shard_map/ppermute | solution.py:365
  6.6 9.8 %collective-permute-done.2.near_b = bf16[1168,128]{1,0:T(8,128)(2,1)S(1)} collective-permute-done((bf16[1168,128]{1,0:T(8,128)(2,1)S(1)}, bf16[1168,128]{1,0:T(8,128)(2,1)S(1)}, u32[]{:S(2)}, u32[]{:S(2)}) %collective-permute-start.2) | collective-permute-done | bytes 299040 | tf_op jit(solution)/shard_map/ppermute | solution.py:365
  16.4 1.5 %collective-permute-start.4 = (bf16[1168,128]{1,0:T(8,128)(2,1)S(1)}, bf16[1168,128]{1,0:T(8,128)(2,1)S(1)}, u32[]{:S(2)}, u32[]{:S(2)}) collective-permute-start(bf16[1168,128]{1,0:T(8,128)(2,1)S(1)} %collective-permute-done.2.near_b), channel_id=1, source_target_pairs={{0,1},{1,0},{2,3},{3,2},{4,5},{5,4},{6,7},{7,6},{8,9},{9,8},{10,11... | collective-permute-start | bytes 897032 | tf_op jit(solution)/shard_map/ppermute | solution.py:365
  18.0 0.0 collective-permute-done.1.near_a
  18.0 0.0 collective-permute-start.3
  18.0 3.1 %collective-permute-start.5 = (bf16[912,128]{1,0:T(8,128)(2,1)S(1)}, bf16[912,128]{1,0:T(8,128)(2,1)S(1)}, u32[]{:S(2)}, u32[]{:S(2)}) collective-permute-start(bf16[912,128]{1,0:T(8,128)(2,1)S(1)} %get-tuple-element.8), channel_id=1, source_target_pairs={{1,4},{3,6},{4,1},{5,8},{6,3},{7,10},{8,5},{9,12},{10,7},{11,14},{... | collective-permute-start | bytes 700424 | tf_op jit(solution)/shard_map/ppermute | solution.py:365
  21.1 10.0 %collective-permute-done.5.far = bf16[912,128]{1,0:T(8,128)(2,1)S(1)} collective-permute-done((bf16[912,128]{1,0:T(8,128)(2,1)S(1)}, bf16[912,128]{1,0:T(8,128)(2,1)S(1)}, u32[]{:S(2)}, u32[]{:S(2)}) %collective-permute-start.5) | collective-permute-done | bytes 233504 | tf_op jit(solution)/shard_map/ppermute | solution.py:365
  31.1 0.0 collective-permute-done.pair
  31.1 0.0 collective-permute-done.4.cross_b
  31.1 0.0 collective-permute-done.3.cross_a
  31.1 13.8 %shard_map.47 = f32[2,13,128,128]{3,2,1,0:T(8,128)} custom-call(s32[2,6]{1,0:T(2,128)} %lists.3, bf16[1168,128]{1,0:T(8,128)(2,1)S(1)} %get-tuple-element.7.own, bf16[1168,128]{1,0:T(8,128)(2,1)S(1)} %collective-permute-done.pair, bf16[1168,128]{1,0:T(8,128)(2,1)S(1)} %collective-permute-done.1.near_a, bf16[1168,128]{1,0:T(8,128)(2,1)S(1)} %collective-permute-done.2.near_b, ...), custom_call_target="tpu_custom_call" | custom-call | flops 12000000000 | bytes 4194304 | tf_op jit(solution)/shard_map/pallas_call | solution.py:392
Async XLA Ops:
  1.1 15.3 %collective-permute-start.2 = (bf16[1168,128]{1,0:T(8,128)(2,1)S(1)}, bf16[1168,128]{1,0:T(8,128)(2,1)S(1)}, u32[]{:S(2)}, u32[]{:S(2)}) collective-permute-start(bf16[1168,128]{1,0:T(8,128)(2,1)S(1)} %get-tuple-element.7.own), channel_id=1, source_target_pairs={{2,4},{3,5},{4,2},{5,3},{6,8},{7,9},{8,6},{9,7},{10,12},{11,13},{1... | collective-permute-start | bytes 897032 | tf_op jit(solution)/shard_map/ppermute | solution.py:365
  5.5 12.5 %collective-permute-start.1 = (bf16[1168,128]{1,0:T(8,128)(2,1)S(1)}, bf16[1168,128]{1,0:T(8,128)(2,1)S(1)}, u32[]{:S(2)}, u32[]{:S(2)}) collective-permute-start(bf16[1168,128]{1,0:T(8,128)(2,1)S(1)} %get-tuple-element.7.own), channel_id=1, source_target_pairs={{0,2},{1,3},{2,0},{3,1},{4,6},{5,7},{6,4},{7,5},{8,10},{9,11},{10,... | collective-permute-start | bytes 897032 | tf_op jit(solution)/shard_map/ppermute | solution.py:365
  5.6 25.5 %collective-permute-start = (bf16[1168,128]{1,0:T(8,128)(2,1)S(1)}, bf16[1168,128]{1,0:T(8,128)(2,1)S(1)}, u32[]{:S(2)}, u32[]{:S(2)}) collective-permute-start(bf16[1168,128]{1,0:T(8,128)(2,1)S(1)} %get-tuple-element.7.own), channel_id=1, source_target_pairs={{0,1},{1,0},{2,3},{3,2},{4,5},{5,4},{6,7},{7,6},{8,9},{9,8},{10,11... | collective-permute-start | bytes 897032 | tf_op jit(solution)/shard_map/ppermute | solution.py:365
  16.4 14.6 %collective-permute-start.4 = (bf16[1168,128]{1,0:T(8,128)(2,1)S(1)}, bf16[1168,128]{1,0:T(8,128)(2,1)S(1)}, u32[]{:S(2)}, u32[]{:S(2)}) collective-permute-start(bf16[1168,128]{1,0:T(8,128)(2,1)S(1)} %collective-permute-done.2.near_b), channel_id=1, source_target_pairs={{0,1},{1,0},{2,3},{3,2},{4,5},{5,4},{6,7},{7,6},{8,9},{9,8},{10,11... | collective-permute-start | bytes 897032 | tf_op jit(solution)/shard_map/ppermute | solution.py:365
  18.0 13.1 %collective-permute-start.3 = (bf16[1168,128]{1,0:T(8,128)(2,1)S(1)}, bf16[1168,128]{1,0:T(8,128)(2,1)S(1)}, u32[]{:S(2)}, u32[]{:S(2)}) collective-permute-start(bf16[1168,128]{1,0:T(8,128)(2,1)S(1)} %collective-permute-done.1.near_a), channel_id=1, source_target_pairs={{0,1},{1,0},{2,3},{3,2},{4,5},{5,4},{6,7},{7,6},{8,9},{9,8},{10,11... | collective-permute-start | bytes 897032 | tf_op jit(solution)/shard_map/ppermute | solution.py:365
  18.0 13.1 %collective-permute-start.5 = (bf16[912,128]{1,0:T(8,128)(2,1)S(1)}, bf16[912,128]{1,0:T(8,128)(2,1)S(1)}, u32[]{:S(2)}, u32[]{:S(2)}) collective-permute-start(bf16[912,128]{1,0:T(8,128)(2,1)S(1)} %get-tuple-element.8), channel_id=1, source_target_pairs={{1,4},{3,6},{4,1},{5,8},{6,3},{7,10},{8,5},{9,12},{10,7},{11,14},{... | collective-permute-start | bytes 700424 | tf_op jit(solution)/shard_map/ppermute | solution.py:365
